TPU v7x, 32 devices: a whole 2x2x4 slice. The times are simulated.
32 devices in a mesh: dp: 2 (over x), tp: 16 (over z, y, core).
Axes of the slice: x: 2, y: 2, z: 4, core: 2. Of those that a mesh axis runs over, the one named last changes fastest.
Arguments:
- x: bfloat16 [16, 384, 2048], P('dp', 'tp'), parts along dimension 0
- k_cache: bfloat16 [16, 4096, 16, 128], P('dp', None, 'tp'), parts along dimension 0
- v_cache: bfloat16 [16, 4096, 16, 128], P('dp', None, 'tp'), parts along dimension 0
- prefix_len: int32 [16], P('dp'), parts along dimension 0
- valid_len: int32 [16], P('dp'), parts along dimension 0
- g_attn: bfloat16 [2048], replicated
- w_q: bfloat16 [2048, 2048], P(None, 'tp')
- b_q: bfloat16 [2048], P('tp')
- w_k: bfloat16 [2048, 2048], P(None, 'tp')
- b_k: bfloat16 [2048], P('tp')
- w_v: bfloat16 [2048, 2048], P(None, 'tp')
- b_v: bfloat16 [2048], P('tp')
- w_o: bfloat16 [2048, 2048], P('tp')
- g_mlp: bfloat16 [2048], replicated
- w_gate: bfloat16 [2048, 5504], P(None, 'tp')
- w_up: bfloat16 [2048, 5504], P(None, 'tp')
- w_down: bfloat16 [5504, 2048], P('tp')
Outputs:
- output 1: bfloat16 [16, 384, 2048], P('dp', 'tp'), parts along dimension 0
- output 2: bfloat16 [16, 4096, 16, 128], P('dp', None, 'tp'), parts along dimension 0
- output 3: bfloat16 [16, 4096, 16, 128], P('dp', None, 'tp'), parts along dimension 0
There are 2 independent parts. A program takes and returns all parts, laid end to end along the dimension named above; an argument that names none is the same for every part.
All inputs are finite; a program needn't handle non-finite values.
Results may differ from a plain program's by a relative error of at most 0.0189305.
Values are sent between devices in bfloat16 or wider.
A program may use at most 1 GiB of HBM per device.

v0:
```python
import jax
import jax.numpy as jnp
from jax import lax
from jax.sharding import PartitionSpec as P

ROPE_THETA = 1.0e6
NORM_EPS = 1.0e-6


def rms_norm(hidden, gain):
    wide_vals = hidden.astype(jnp.float32)
    inv_rms = lax.rsqrt(jnp.mean(wide_vals * wide_vals, axis=-1, keepdims=True) + NORM_EPS)
    return (wide_vals * inv_rms * gain.astype(jnp.float32)).astype(jnp.bfloat16)


def rotate_heads(heads, positions):
    half = heads.shape[-1] // 2
    inv_freq = ROPE_THETA ** (-(jnp.arange(half, dtype=jnp.float32) * 2.0) / heads.shape[-1])
    angles = positions.astype(jnp.float32)[..., None] * inv_freq
    cos_t = jnp.cos(angles)[..., None, :]
    sin_t = jnp.sin(angles)[..., None, :]
    wide = heads.astype(jnp.float32)
    first_half = wide[..., :half]
    second_half = wide[..., half:]
    rotated = jnp.concatenate([first_half * cos_t - second_half * sin_t, second_half * cos_t + first_half * sin_t], axis=-1)
    return rotated.astype(jnp.bfloat16)


def project(hidden, weight, bias):
    total = jnp.einsum("rcd,dn->rcn", hidden, weight, preferred_element_type=jnp.float32)
    return (total + bias.astype(jnp.float32)).astype(jnp.bfloat16)


def write_rows(cache, new_rows, prefix, valid):
    n_tokens = new_rows.shape[1]
    row_ids = jnp.arange(n_tokens, dtype=jnp.int32)[None, :, None, None]
    window = (1, n_tokens, cache.shape[2], cache.shape[3])

    def body(req_idx, buffer):
        start = prefix[req_idx]
        old_rows = lax.dynamic_slice(buffer, (req_idx, start, 0, 0), window)
        fresh = lax.dynamic_slice_in_dim(new_rows, req_idx, 1, axis=0)
        merged = jnp.where(row_ids < valid[req_idx], fresh, old_rows)
        return lax.dynamic_update_slice(buffer, merged, (req_idx, start, 0, 0))

    return lax.fori_loop(0, cache.shape[0], body, cache)


def attend(queries, k_cache, v_cache, prefix, valid):
    n_req, n_tokens, q_heads, head_dim = queries.shape
    slots, kv_local = k_cache.shape[1], k_cache.shape[2]
    query_groups = queries.reshape(n_req, n_tokens, kv_local, q_heads // kv_local, head_dim)
    scores = jnp.einsum("rckgd,rskd->rkgcs", query_groups, k_cache, preferred_element_type=jnp.float32) * (head_dim ** -0.5)
    row_ids = jnp.arange(n_tokens, dtype=jnp.int32)
    limit = prefix[:, None] + jnp.minimum(row_ids[None, :], valid[:, None] - 1)
    visible = jnp.arange(slots, dtype=jnp.int32)[None, None, :] <= limit[:, :, None]
    scores = jnp.where(visible[:, None, None], scores, -1.0e30)
    attn_probs = jax.nn.softmax(scores, axis=-1).astype(jnp.bfloat16)
    mixed = jnp.einsum("rkgcs,rskd->rckgd", attn_probs, v_cache, preferred_element_type=jnp.float32)
    return mixed.astype(jnp.bfloat16).reshape(n_req, n_tokens, q_heads * head_dim)


def attention_heads(normed_full, k_cache, v_cache, prefix, valid, w_q, b_q, w_k, b_k, w_v, b_v):
    n_req, n_tokens = normed_full.shape[0], normed_full.shape[1]
    head_dim = k_cache.shape[-1]
    positions = prefix[:, None] + jnp.arange(n_tokens, dtype=jnp.int32)[None, :]
    queries = rotate_heads(project(normed_full, w_q, b_q).reshape(n_req, n_tokens, -1, head_dim), positions)
    keys_new = rotate_heads(project(normed_full, w_k, b_k).reshape(n_req, n_tokens, -1, head_dim), positions)
    values_new = project(normed_full, w_v, b_v).reshape(n_req, n_tokens, -1, head_dim)
    k_out = write_rows(k_cache, keys_new, prefix, valid)
    v_out = write_rows(v_cache, values_new, prefix, valid)
    return attend(queries, k_out, v_out, prefix, valid), k_out, v_out


def mlp_partial(normed_full, w_gate, w_up, w_down):
    gate = jnp.einsum("rcd,df->rcf", normed_full, w_gate, preferred_element_type=jnp.float32)
    up_proj = jnp.einsum("rcd,df->rcf", normed_full, w_up, preferred_element_type=jnp.float32)
    hidden_act = (jax.nn.silu(gate) * up_proj).astype(jnp.bfloat16)
    return jnp.einsum("rcf,fd->rcd", hidden_act, w_down, preferred_element_type=jnp.float32).astype(jnp.bfloat16)


def add_rounded(first, second):
    return (first.astype(jnp.float32) + second.astype(jnp.float32)).astype(jnp.bfloat16)


def solution(mesh):
    row_spec = P("dp", "tp", None)
    cache_spec = P("dp", None, "tp", None)
    req_spec = P("dp")
    rep_spec = P(None)
    col_spec = P(None, "tp")
    bias_spec = P("tp")
    down_spec = P("tp", None)

    def layer(x_rows, k_cache, v_cache, prefix, valid, g_attn, w_q, b_q, w_k, b_k, w_v, b_v, w_o, g_mlp, w_gate, w_up, w_down):
        normed = rms_norm(x_rows, g_attn)
        normed_full = lax.all_gather(normed, "tp", axis=1, tiled=True)
        attended, k_out, v_out = attention_heads(normed_full, k_cache, v_cache, prefix, valid, w_q, b_q, w_k, b_k, w_v, b_v)
        attn_part = jnp.einsum("rcn,nd->rcd", attended, w_o, preferred_element_type=jnp.float32).astype(jnp.bfloat16)
        attn_rows = lax.psum_scatter(attn_part, "tp", scatter_dimension=1, tiled=True)
        resid_mid = add_rounded(x_rows, attn_rows)
        normed_mlp = rms_norm(resid_mid, g_mlp)
        mlp_full = lax.all_gather(normed_mlp, "tp", axis=1, tiled=True)
        down_part = mlp_partial(mlp_full, w_gate, w_up, w_down)
        down_rows = lax.psum_scatter(down_part, "tp", scatter_dimension=1, tiled=True)
        return add_rounded(resid_mid, down_rows), k_out, v_out

    in_specs = (row_spec, cache_spec, cache_spec, req_spec, req_spec, rep_spec, col_spec, bias_spec, col_spec, bias_spec, col_spec, bias_spec, down_spec, rep_spec, col_spec, col_spec, down_spec)
    return jax.shard_map(layer, mesh=mesh, in_specs=in_specs, out_specs=(row_spec, cache_spec, cache_spec), check_vma=False)
```

profile of v0, /device:TPU:0, one launch (start us, length us, event | category | flops | bytes accessed | tf_op | source)
XLA Modules:
  0.0 744.6 jit_solution(12535089210600926834)
XLA Ops:
  7.2 7.5 %copy.89 = bf16[8,4096,1,128]{3,1,2,0:T(8,128)(2,1)} copy(bf16[8,4096,1,128]{3,1,2,0:T(8,128)(2,1)} %param.22) | data formatting | bytes 16777216
  14.8 7.5 %copy.90 = bf16[8,4096,1,128]{3,1,2,0:T(8,128)(2,1)} copy(bf16[8,4096,1,128]{3,1,2,0:T(8,128)(2,1)} %param.23) | data formatting | bytes 16777216
  23.9 102.8 %all-gather.3.cloned.1.call-done = bf16[8,384,2048]{2,1,0:T(8,128)(2,1)} async-done(((bf16[8,24,2048]{2,1,0:T(8,128)(2,1)}), bf16[8,384,2048]{2,1,0:T(8,128)(2,1)}) %all-gather.3.cloned.1.call-update) | async-done | bytes 12582928 | tf_op jit(solution)/shard_map/all_gather | solution.py:97
  126.7 10.2 %fusion.32 = f32[8,384,1,128]{1,3,0,2:T(8,128)} fusion(bf16[8,384,2048]{2,1,0:T(8,128)(2,1)} %all-gather.3.cloned.1.call-done, f32[128]{0:T(128)S(1)} %convert_element_type.115, bf16[2048,128]{1,0:T(8,128)(2,1)S(1)} %copy-done.3), kind=kOutput, calls=%fused_computation.47 | convolution fusion | flops 1611792384 | bytes 14680576 | tf_op jit(solution)/shard_map/rcd,dn->rcn/dot_general | solution.py:30
  136.9 5.4 fusion.30
  142.3 6.0 fusion.62
  148.4 52.3 %while.29 = (s32[]{:T(128)}, bf16[8,4096,1,128]{3,1,2,0:T(8,128)(2,1)}, s32[8]{0:T(128)S(1)}, bf16[8,384,1,128]{1,3,0,2:T(8,128)(2,1)S(1)}, s32[8]{0:T(128)S(1)}, /*index=5*/s32[]{:T(128)}, s32[]{:T(128)}, s32[]{:T(128)}) while((s32[]{:T(128)}, bf16[8,4096,1,128]{3,1,2,0:T(8,128)(2,1)}, s32[8]{0:T(128)S(1)}, ...), condition=%wide.region_4.5_spmd.clone, body=%wide.region_3.4_spmd.clone.sunk | while | flops 49541 | bytes 885675 | solution.py:46
  166.3 1.7 dynamic_update_slice.19
  199.0 1.7 dynamic_update_slice.19
  200.7 9.0 %fusion.28 = bf16[8,384,1,128]{3,1,2,0:T(8,128)(2,1)} fusion(bf16[8,384,2048]{2,1,0:T(8,128)(2,1)} %all-gather.3.cloned.1.call-done, f32[128]{0:T(128)S(1)} %convert_element_type.108, bf16[2048,128]{1,0:T(8,128)(2,1)} %param.31), kind=kOutput, calls=%fused_computation.43 | convolution fusion | flops 1611399168 | bytes 13894144 | tf_op jit(solution)/shard_map/rcd,dn->rcn/dot_general | solution.py:30
  209.7 52.4 %while.28 = (s32[]{:T(128)}, bf16[8,4096,1,128]{3,1,2,0:T(8,128)(2,1)}, s32[8]{0:T(128)S(1)}, bf16[8,384,1,128]{3,1,2,0:T(8,128)(2,1)}, s32[8]{0:T(128)S(1)}, /*index=5*/s32[]{:T(128)}, s32[]{:T(128)}, s32[]{:T(128)}) while((s32[]{:T(128)}, bf16[8,4096,1,128]{3,1,2,0:T(8,128)(2,1)}, s32[8]{0:T(128)S(1)}, ...), condition=%wide.region_2.3_spmd.clone, body=%wide.region_1.2_spmd.clone.sunk | while | flops 49541 | bytes 492455 | solution.py:46
  262.2 22.2 %fusion.5 = (f32[8,384]{1,0:T(8,128)S(1)}, f32[8,4096,384]{2,1,0:T(8,128)}) fusion(s32[8,384]{1,0:T(8,128)S(1)} %get-tuple-element.303, bf16[8,384,64]{1,2,0:T(8,128)(2,1)S(1)} %copy-done.7, bf16[8,384,64]{1,2,0:T(8,128)(2,1)S(1)} %copy-done.6, bf16[8,4096,1,128]{3,1,2,0:T(8,128)(2,1)} %get-tuple-element.219), kind=kOutput, calls=%fused_computation.12 | convolution fusion | flops 3273126912 | bytes 59531264 | tf_op jit(solution)/shard_map/rckgd,rskd->rkgcs/dot_general | solution.py:53
  284.4 21.8 %fusion.4 = f32[8,384]{1,0:T(8,128)S(1)} fusion(f32[8,4096,384]{2,1,0:T(8,128)} %get-tuple-element.306, f32[8,384]{1,0:T(8,128)S(1)} %get-tuple-element.305, s32[8,384]{1,0:T(8,128)S(1)} %get-tuple-element.303), kind=kLoop, calls=%fused_computation.11 | loop fusion | flops 62911488 | bytes 50368512 | tf_op jit(solution)/shard_map/reduce_sum | solution.py:58
  306.2 24.6 %fusion.33 = bf16[8,384,128]{1,2,0:T(8,128)(2,1)S(1)} fusion(f32[8,384]{1,0:T(8,128)S(1)} %fusion.4, f32[8,384]{1,0:T(8,128)S(1)} %get-tuple-element.305, f32[8,4096,384]{2,1,0:T(8,128)} %get-tuple-element.306, s32[8,384]{1,0:T(8,128)S(1)} %get-tuple-element.303, bf16[8,4096,1,128]{3,1,2,0:T(8,128)(2,1)} %get-tuple-element.220), kind=kOutput, calls=%fused_computation.48 | convolution fusion | flops 3297116160 | bytes 59543552 | tf_op jit(solution)/shard_map/rkgcs,rskd->rckgd/dot_general | solution.py:59
  330.8 3.7 fusion.69
  334.5 5.1 copy.57
  340.2 131.3 %reduce-scatter.7.cloned.1.call-done = bf16[24,16384]{1,0:T(8,128)(2,1)} async-done(((bf16[384,16384]{1,0:T(8,128)(2,1)}), bf16[24,16384]{1,0:T(8,128)(2,1)}) %reduce-scatter.7.cloned.1.call-update) | async-done | bytes 786448
  475.4 99.8 %all-gather.5.cloned.1.call-done = bf16[8,384,2048]{2,1,0:T(8,128)(2,1)} async-done(((bf16[8,24,2048]{2,1,0:T(8,128)(2,1)}), bf16[8,384,2048]{2,1,0:T(8,128)(2,1)}) %all-gather.5.cloned.1.call-update) | async-done | bytes 12582928 | tf_op jit(solution)/shard_map/all_gather | solution.py:103
  575.2 9.2 %fusion.20 = f32[8,384,344]{1,2,0:T(8,128)S(1)} fusion(bf16[8,384,2048]{2,1,0:T(8,128)(2,1)} %all-gather.5.cloned.1.call-done, bf16[2048,344]{0,1:T(8,128)(2,1)} %param.36), kind=kOutput, calls=%fused_computation.39 | convolution fusion | flops 4328521728 | bytes 18219008 | tf_op jit(solution)/shard_map/rcd,df->rcf/dot_general | solution.py:77
  584.4 5.4 multiply_convert_fusion
  589.8 7.1 fusion.66
  596.9 5.4 copy.59
  602.3 132.0 %reduce-scatter.9.cloned.1.call-done = bf16[24,16384]{1,0:T(8,128)(2,1)} async-done(((bf16[384,16384]{1,0:T(8,128)(2,1)}), bf16[24,16384]{1,0:T(8,128)(2,1)}) %reduce-scatter.9.cloned.1.call-update) | async-done | bytes 786448
  735.8 1.8 fusion.18
  (153 shorter events, 78.4 us)
Async XLA Ops:
  7.2 582.6 %copy-start = (bf16[344,2048]{1,0:T(8,128)(2,1)S(1)}, bf16[344,2048]{1,0:T(8,128)(2,1)}, u32[]{:S(2)}) copy-start(bf16[344,2048]{1,0:T(8,128)(2,1)} %param.37) | copy-start | bytes 4227076
  7.2 119.5 %all-gather.3.cloned.1.call-start = ((), (), s32[]{:S(2)}) async-start(), calls=%async_computation.2 | async-start | bytes 13369344 | tf_op jit(solution)/shard_map/all_gather | solution.py:97
  14.7 7.5 %copy-start.2 = (bf16[8,24,2048]{2,1,0:T(8,128)(2,1)S(1)}, bf16[8,24,2048]{2,1,0:T(8,128)(2,1)}, u32[]{:S(2)}) copy-start(bf16[8,24,2048]{2,1,0:T(8,128)(2,1)} %param.21) | copy-start | bytes 2359300
  14.7 7.8 %copy-start.8 = (bf16[2048]{0:T(1024)(128)(2,1)S(1)}, bf16[2048]{0:T(1024)(128)(2,1)}, u32[]{:S(2)}) copy-start(bf16[2048]{0:T(1024)(128)(2,1)} %param.26) | copy-start | bytes 12292
  14.7 9.0 %copy-start.13 = (bf16[128]{0:T(256)(128)(2,1)S(1)}, bf16[128]{0:T(256)(128)(2,1)}, u32[]{:S(2)}) copy-start(bf16[128]{0:T(256)(128)(2,1)} %param.28) | copy-start | bytes 772
  14.7 9.0 %copy-start.14 = (bf16[128]{0:T(256)(128)(2,1)S(1)}, bf16[128]{0:T(256)(128)(2,1)}, u32[]{:S(2)}) copy-start(bf16[128]{0:T(256)(128)(2,1)} %param.30) | copy-start | bytes 772
  14.7 9.0 %copy-start.15 = (bf16[128]{0:T(256)(128)(2,1)S(1)}, bf16[128]{0:T(256)(128)(2,1)}, u32[]{:S(2)}) copy-start(bf16[128]{0:T(256)(128)(2,1)} %param.32) | copy-start | bytes 772
  14.7 9.1 %copy-start.16 = (s32[8]{0:T(128)S(1)}, s32[8]{0:T(128)}, u32[]{:S(2)}) copy-start(s32[8]{0:T(128)} %param.25) | copy-start | bytes 100
  14.7 9.1 %copy-start.10 = (s32[8]{0:T(128)S(1)}, s32[8]{0:T(128)}, u32[]{:S(2)}) copy-start(s32[8]{0:T(128)} %param.24) | copy-start | bytes 100
  14.8 111.9 %copy-start.3 = (bf16[2048,128]{1,0:T(8,128)(2,1)S(1)}, bf16[2048,128]{1,0:T(8,128)(2,1)}, u32[]{:S(2)}) copy-start(bf16[2048,128]{1,0:T(8,128)(2,1)} %param.27) | copy-start | bytes 1572868
  22.5 114.3 %copy-start.4 = (bf16[2048,128]{1,0:T(8,128)(2,1)S(1)}, bf16[2048,128]{1,0:T(8,128)(2,1)}, u32[]{:S(2)}) copy-start(bf16[2048,128]{1,0:T(8,128)(2,1)} %param.29) | copy-start | bytes 1572868
  23.7 447.8 %reduce-scatter.7.cloned.1.call-start = ((), (), s32[]{:S(2)}) async-start(), calls=%async_computation.4 | async-start | bytes 13369344
  126.7 10.2 %copy-start.1 = (bf16[8,384,2048]{2,1,0:T(8,128)(2,1)S(1)}, bf16[8,384,2048]{2,1,0:T(8,128)(2,1)}, u32[]{:S(2)}) copy-start(bf16[8,384,2048]{2,1,0:T(8,128)(2,1)} %all-gather.3.cloned.1.call-done) | copy-start | bytes 37748740
  200.7 61.5 %copy-start.6 = (bf16[8,384,64]{1,2,0:T(8,128)(2,1)S(1)}, bf16[8,384,64]{1,2,0:T(8,128)(2,1)}, u32[]{:S(2)}) copy-start(bf16[8,384,64]{1,2,0:T(8,128)(2,1)} %get-tuple-element.297) | copy-start | bytes 1179652
  200.7 61.5 %copy-start.7 = (bf16[8,384,64]{1,2,0:T(8,128)(2,1)S(1)}, bf16[8,384,64]{1,2,0:T(8,128)(2,1)}, u32[]{:S(2)}) copy-start(bf16[8,384,64]{1,2,0:T(8,128)(2,1)} %get-tuple-element.298) | copy-start | bytes 1179652
  306.2 24.6 %copy-start.5 = (bf16[128,2048]{1,0:T(8,128)(2,1)S(1)}, bf16[128,2048]{1,0:T(8,128)(2,1)}, u32[]{:S(2)}) copy-start(bf16[128,2048]{1,0:T(8,128)(2,1)} %param.33) | copy-start | bytes 1572868
  339.5 0.7 copy-start.9
  339.6 235.6 %all-gather.5.cloned.1.call-start = ((), (), s32[]{:S(2)}) async-start(), calls=%async_computation.3 | async-start | bytes 13369344 | tf_op jit(solution)/shard_map/all_gather | solution.py:103
  475.3 258.9 %reduce-scatter.9.cloned.1.call-start = ((), (), s32[]{:S(2)}) async-start(), calls=%async_computation.5 | async-start | bytes 13369344
  575.2 9.2 %copy-start.11 = (bf16[8,384,2048]{2,1,0:T(8,128)(2,1)S(1)}, bf16[8,384,2048]{2,1,0:T(8,128)(2,1)}, u32[]{:S(2)}) copy-start(bf16[8,384,2048]{2,1,0:T(8,128)(2,1)} %all-gather.5.cloned.1.call-done) | copy-start | bytes 37748740
  575.2 9.2 %copy-start.12 = (bf16[2048,344]{0,1:T(8,128)(2,1)S(1)}, bf16[2048,344]{0,1:T(8,128)(2,1)}, u32[]{:S(2)}) copy-start(bf16[2048,344]{0,1:T(8,128)(2,1)} %param.35) | copy-start | bytes 4227076
Sparse Core Ops, SparseCore 0:
  23.8 102.8 all-gather.2
  339.7 131.7 reduce-scatter.6
  475.4 99.6 all-gather.4
  602.4 131.7 reduce-scatter.8
where the time goes:
time: 753 us; the launch traced here: 745 us
  waiting for transfers between devices  466 us (62%)
  matrix products  96.7 us (13%)
  local copies, waits for them, and re-layouts  76.8 us (10%)
  other arithmetic  59.8 us (8%)
  loops' own time  30.8 us (4%)
  between operations  14.5 us (2%)
    unnamed x6, waiting for transfers between devices  263 us
    all_gather x1, waiting for transfers between devices, layer(): normed_full = lax.all_gather(normed, 'tp', axis=1, tiled=True)  103 us
    all_gather x1, waiting for transfers between devices, layer(): mlp_full = lax.all_gather(normed_mlp, 'tp', axis=1, tiled=True)  99.8 us
    another operation x2, loops' own time, write_rows(): return lax.fori_loop(0, cache.shape[0], body, cache)  30.8 us
    unnamed x40, local copies, waits for them, and re-layouts  29.3 us
    dynamic_update_slice x16, local copies, waits for them, and re-layouts, body(): return lax.dynamic_update_slice(buffer, merged, (req_idx, start, 0, 0))  27.3 us
    dot_general x3, matrix products, project(): jnp.einsum('rcd,dn->rcn', hidden, weight, preferred_element_type=jnp.floa...  24.6 us
    dot_general x1, matrix products, attend(): jnp.einsum('rkgcs,rskd->rckgd', attn_probs, v_cache, preferred_element_ty...  24.6 us
  transfers between devices with their start and end apart: 4, of which 4 were waited for; matrix products, arithmetic and copies ran while one was open for 0% of the time, Pallas kernels for 0%

commit v1 on v0

v1 whole, which is shorter than its diff:
```python
import functools
import jax
import jax.numpy as jnp
from jax import lax
from jax.experimental import pallas as pl
from jax.experimental.pallas import tpu as pltpu
from jax.sharding import PartitionSpec as P

ROPE_THETA = 1.0e6
NORM_EPS = 1.0e-6
KV_BLOCK = 512
UPDATE_ROWS = 400
LOG2_E = 1.4426950408889634


MESH_ID = pl.DeviceIdType.MESH
LINE = 4
CHUNKS = 4
TO_UPPER, TO_LOWER, TO_OTHER_LINE, TO_TWIN = range(4)
ARRIVAL = ((0, 1, 2, 3), (1, 0, 2, 3), (2, 1, 3, 0), (3, 2, 1, 0))


def scaled_norm(wide_vals, gain):
    inv_rms = lax.rsqrt(jnp.mean(wide_vals * wide_vals, axis=-1, keepdims=True) + NORM_EPS)
    return (wide_vals * inv_rms * gain).astype(jnp.bfloat16)


def place():
    me = lax.axis_index("tp")
    return lax.axis_index("dp"), me // 4, (me // 2) % 2, me % 2


def chip_at(table, z, m):
    packed = [sum(v << (2 * i) for i, v in enumerate(row)) for row in table]
    code = jnp.where(z == 0, packed[0], jnp.where(z == 1, packed[1], jnp.where(z == 2, packed[2], packed[3])))
    return (code >> (2 * m)) & 3


def greet(devices_of):
    dp, z, y, c = devices_of
    barrier = pltpu.get_barrier_semaphore()

    @pl.when(z > 0)
    def _():
        pl.semaphore_signal(barrier, 1, device_id=(dp, (z - 1) * 4 + y * 2 + c), device_id_type=MESH_ID)

    @pl.when(z < LINE - 1)
    def _():
        pl.semaphore_signal(barrier, 1, device_id=(dp, (z + 1) * 4 + y * 2 + c), device_id_type=MESH_ID)

    pl.semaphore_signal(barrier, 1, device_id=(dp, z * 4 + (1 - y) * 2 + c), device_id_type=MESH_ID)
    pl.semaphore_signal(barrier, 1, device_id=(dp, z * 4 + y * 2 + 1 - c), device_id_type=MESH_ID)
    pl.semaphore_wait(barrier, 2 + (z + 3) // 4 + (6 - z) // 4)


class RowGather:
    def __init__(self, buf, send_sem, recv_sem, where):
        self.buf, self.send_sem, self.recv_sem = buf, send_sem, recv_sem
        self.dp, self.z, self.y, self.c = where
        self.rows = buf.shape[0] // 16
        self.piece = self.rows // CHUNKS

    def copy(self, block, j, way, device):
        rows = pl.ds(pl.multiple_of(block * self.rows + j * self.piece, 16), self.piece)
        return pltpu.make_async_remote_copy(
            src_ref=self.buf.at[rows],
            dst_ref=self.buf.at[rows],
            send_sem=self.send_sem.at[way],
            recv_sem=self.recv_sem.at[block * CHUNKS + j],
            device_id=(self.dp, device),
            device_id_type=MESH_ID,
        )

    def arrived(self, block, j):
        self.copy(block, j, 0, 0).wait_recv()

    def spread(self, block, j, zc, ups):
        y, c = self.y, self.c
        if ups[0] and zc < LINE - 1:
            self.copy(block, j, TO_UPPER, (zc + 1) * 4 + y * 2 + c).start()
        if ups[1] and zc > 0:
            self.copy(block, j, TO_LOWER, (zc - 1) * 4 + y * 2 + c).start()
        self.copy(block, j, TO_OTHER_LINE, zc * 4 + (1 - y) * 2 + c).start()
        self.copy(block, j, TO_TWIN, zc * 4 + y * 2 + 1 - c).start()

    def across(self, zc, m):
        y, c = self.y, self.c
        block = ARRIVAL[zc][m] * 4 + (1 - y) * 2 + c
        for j in range(CHUNKS):
            self.arrived(block, j)
            self.copy(block, j, TO_TWIN, zc * 4 + y * 2 + 1 - c).start()

    def early(self):
        for zc in range(LINE):

            @pl.when(self.z == zc)
            def _(zc=zc):
                y, c = self.y, self.c
                for j in range(CHUNKS):
                    self.spread(zc * 4 + y * 2 + c, j, zc, (True, True))
                for far in range(1, LINE):
                    for j in range(CHUNKS):
                        if zc - far >= 0:
                            block = (zc - far) * 4 + y * 2 + c
                            self.arrived(block, j)
                            self.spread(block, j, zc, (True, False))
                        if zc + far < LINE:
                            block = (zc + far) * 4 + y * 2 + c
                            self.arrived(block, j)
                            self.spread(block, j, zc, (False, True))
                    self.across(zc, far - 1)

    def late(self):
        for zc in range(LINE):

            @pl.when(self.z == zc)
            def _(zc=zc):
                self.across(zc, LINE - 1)

    def twin_arrived(self, block):
        for j in range(CHUNKS):
            self.arrived(block, j)

    def drain(self):
        def sent(way, blocks):
            rows = pl.ds(0, blocks * self.rows)
            pltpu.make_async_remote_copy(
                src_ref=self.buf.at[rows],
                dst_ref=self.buf.at[rows],
                send_sem=self.send_sem.at[way],
                recv_sem=self.recv_sem.at[0],
                device_id=(self.dp, 0),
                device_id_type=MESH_ID,
            ).wait_send()

        for zc in range(LINE):

            @pl.when(self.z == zc)
            def _(zc=zc):
                if zc < LINE - 1:
                    sent(TO_UPPER, zc + 1)
                if zc > 0:
                    sent(TO_LOWER, LINE - zc)

        sent(TO_OTHER_LINE, LINE)
        sent(TO_TWIN, 2 * LINE)


def project_body(x_ref, gain_ref, w_ref, bias_ref, base_cos_ref, base_sin_ref, step_cos_ref, step_sin_ref, q_ref, k_ref, v_ref, rows_buf, send_sem, recv_sem):
    where = place()
    dp, z, y, c = where
    rows = x_ref.shape[0]
    head_dim = q_ref.shape[1]
    own_tokens = step_cos_ref.shape[0] // 16
    me = z * 4 + y * 2 + c
    own = pl.ds(pl.multiple_of(me * rows, 16), rows)
    rows_buf[own, :] = scaled_norm(x_ref[...].astype(jnp.float32), gain_ref[...].astype(jnp.float32))
    greet(where)
    gather = RowGather(rows_buf, send_sem, recv_sem, where)
    gather.early()

    def compute(block):
        at = pl.ds(pl.multiple_of(block * rows, 16), rows)
        out = jnp.dot(rows_buf[at, :], w_ref[...], preferred_element_type=jnp.float32)
        out = (out + bias_ref[...].astype(jnp.float32)).astype(jnp.bfloat16)
        steps = pl.ds(pl.multiple_of(block * own_tokens, 8), own_tokens)
        step_cos, step_sin = step_cos_ref[steps, :][None], step_sin_ref[steps, :][None]
        base_cos, base_sin = base_cos_ref[...][:, None, :], base_sin_ref[...][:, None, :]
        cos_t = (base_cos * step_cos - base_sin * step_sin).reshape(rows, head_dim)
        sin_t = (base_sin * step_cos + base_cos * step_sin).reshape(rows, head_dim)
        lane = lax.broadcasted_iota(jnp.int32, (rows, head_dim), 1)
        sin_t = jnp.where(lane < head_dim // 2, -sin_t, sin_t)
        for ref, i in ((q_ref, 0), (k_ref, 1)):
            wide = out[:, i * head_dim:(i + 1) * head_dim].astype(jnp.float32)
            ref[at, :] = (wide * cos_t + pltpu.roll(wide, head_dim // 2, 1) * sin_t).astype(jnp.bfloat16)
        v_ref[at, :] = out[:, 2 * head_dim:]

    def chip(place_z, line):
        compute(place_z * 4 + line * 2 + c)
        twin = place_z * 4 + line * 2 + 1 - c
        gather.twin_arrived(twin)
        compute(twin)

    @pl.loop(0, 6)
    def _(m):
        chip(chip_at(ARRIVAL, z, m % 4), (y + m // 4) % 2)

    gather.late()

    @pl.loop(2, 4)
    def _(m):
        chip(chip_at(ARRIVAL, z, m), 1 - y)

    gather.drain()


def project_all(x_rows, gain, w_all, bias_all, prefix):
    n_req, own_tokens, width = x_rows.shape
    rows = n_req * own_tokens
    head_dim = w_all.shape[1] // 3
    half = head_dim // 2
    inv_freq = ROPE_THETA ** (-(jnp.arange(half, dtype=jnp.float32) * 2.0) / head_dim)
    inv_freq = jnp.concatenate([inv_freq, inv_freq])[None, :]
    base = prefix.astype(jnp.float32)[:, None] * inv_freq
    step = jnp.arange(16 * own_tokens, dtype=jnp.float32)[:, None] * inv_freq
    vmem = pl.BlockSpec(memory_space=pltpu.VMEM)
    out = jax.ShapeDtypeStruct((16 * rows, head_dim), jnp.bfloat16)
    outs = pl.pallas_call(
        project_body,
        out_shape=(out, out, out),
        in_specs=[vmem] * 8,
        out_specs=(vmem,) * 3,
        scratch_shapes=[
            pltpu.VMEM((16 * rows, width), jnp.bfloat16),
            pltpu.SemaphoreType.DMA((4,)),
            pltpu.SemaphoreType.DMA((16 * CHUNKS,)),
        ],
        compiler_params=pltpu.CompilerParams(collective_id=0, has_side_effects=True, vmem_limit_bytes=40 * 2**20),
        cost_estimate=pl.CostEstimate(flops=2 * 16 * rows * width * 3 * head_dim, bytes_accessed=4 * rows * width, transcendentals=0),
        name="project",
    )(x_rows.reshape(rows, width), gain[None, :], w_all, bias_all[None, :], jnp.cos(base), jnp.sin(base), jnp.cos(step), jnp.sin(step))
    return tuple(o.reshape(16, n_req, own_tokens, head_dim) for o in outs)


def token_rows(ref):
    rows = ref[:, 0].astype(jnp.float32)
    return rows.reshape(rows.shape[0] * rows.shape[1], rows.shape[2])


def attention_body(prefix_ref, valid_ref, q_ref, kn_ref, vn_ref, k_ref, v_ref, o_ref, ko_ref, vo_ref, scores, top, total, acc):
    req = pl.program_id(0)
    start = prefix_ref[req]
    count = valid_ref[req]
    head_dim = q_ref.shape[3]
    n_tokens = q_ref.shape[0] * q_ref.shape[2]
    slots = k_ref.shape[1]
    ko_ref[...] = k_ref[...]
    vo_ref[...] = v_ref[...]
    base = pl.multiple_of(jnp.minimum((start // 16) * 16, slots - UPDATE_ROWS), 16)
    shift = start - base
    row = lax.broadcasted_iota(jnp.int32, (UPDATE_ROWS, head_dim), 0) - shift
    keep = (row >= 0) & (row < count)
    for src, dst in ((kn_ref, ko_ref), (vn_ref, vo_ref)):
        fresh = jnp.concatenate([token_rows(src), jnp.zeros((UPDATE_ROWS - n_tokens, head_dim), jnp.float32)], axis=0)
        fresh = pltpu.roll(fresh, shift, 0)
        old = dst[0, pl.ds(base, UPDATE_ROWS), :].astype(jnp.float32)
        dst[0, pl.ds(base, UPDATE_ROWS), :] = jnp.where(keep, fresh, old).astype(jnp.bfloat16)

    n_open = (start + 1) // KV_BLOCK
    n_used = pl.cdiv(start + count, KV_BLOCK)
    queries = token_rows(q_ref).astype(jnp.bfloat16)
    lanes = KV_BLOCK // 128
    top[...] = jnp.full_like(top, -1.0e30)

    def score(blk, masked):
        keys = ko_ref[0, pl.ds(pl.multiple_of(blk * KV_BLOCK, KV_BLOCK), KV_BLOCK), :]
        s = lax.dot_general(queries, keys, (((1,), (1,)), ((), ())), preferred_element_type=jnp.float32)
        if masked:
            col = lax.broadcasted_iota(jnp.int32, (n_tokens, KV_BLOCK), 1) + blk * KV_BLOCK
            row_id = lax.broadcasted_iota(jnp.int32, (n_tokens, KV_BLOCK), 0)
            s = jnp.where(col <= start + jnp.minimum(row_id, count - 1), s, -1.0e30)
        scores[blk] = s
        best = top[...]
        for j in range(lanes):
            best = jnp.maximum(best, s[:, j * 128:(j + 1) * 128])
        top[...] = best

    pl.loop(0, n_open)(lambda blk: score(blk, False))
    pl.loop(n_open, n_used)(lambda blk: score(blk, True))
    top[...] = jnp.broadcast_to(jnp.max(top[...], axis=1, keepdims=True), top.shape)
    total[...] = jnp.zeros_like(total)
    acc[...] = jnp.zeros_like(acc)

    @pl.loop(0, n_used)
    def _(blk):
        best = top[...]
        part = total[...]
        pieces = []
        for j in range(lanes):
            e = jnp.exp2((scores[blk, :, j * 128:(j + 1) * 128] - best) * (LOG2_E * head_dim ** -0.5))
            part = part + e
            pieces.append(e.astype(jnp.bfloat16))
        total[...] = part
        vals = vo_ref[0, pl.ds(pl.multiple_of(blk * KV_BLOCK, KV_BLOCK), KV_BLOCK), :]
        acc[...] += jnp.dot(jnp.concatenate(pieces, axis=1), vals, preferred_element_type=jnp.float32)

    mixed = acc[...] / jnp.sum(total[...], axis=1, keepdims=True)
    o_ref[:, 0] = mixed.reshape(o_ref.shape[0], o_ref.shape[2], head_dim).astype(jnp.bfloat16)


def attend(queries, keys_new, values_new, k_cache, v_cache, prefix, valid):
    owners, n_req, own_tokens, head_dim = queries.shape
    n_tokens = owners * own_tokens
    slots = k_cache.shape[1]
    new_spec = pl.BlockSpec((owners, 1, own_tokens, head_dim), lambda r, *_: (0, r, 0, 0))
    cache_spec = pl.BlockSpec((1, slots, head_dim), lambda r, *_: (r, 0, 0))
    cache_out = jax.ShapeDtypeStruct(k_cache.shape, jnp.bfloat16)
    return pl.pallas_call(
        attention_body,
        out_shape=(jax.ShapeDtypeStruct(queries.shape, jnp.bfloat16), cache_out, cache_out),
        grid_spec=pltpu.PrefetchScalarGridSpec(
            num_scalar_prefetch=2,
            grid=(n_req,),
            in_specs=[new_spec, new_spec, new_spec, cache_spec, cache_spec],
            out_specs=(new_spec, cache_spec, cache_spec),
            scratch_shapes=[
                pltpu.VMEM((slots // KV_BLOCK, n_tokens, KV_BLOCK), jnp.float32),
                pltpu.VMEM((n_tokens, 128), jnp.float32),
                pltpu.VMEM((n_tokens, 128), jnp.float32),
                pltpu.VMEM((n_tokens, head_dim), jnp.float32),
            ],
        ),
        compiler_params=pltpu.CompilerParams(dimension_semantics=("arbitrary",), vmem_limit_bytes=40 * 2**20),
        cost_estimate=pl.CostEstimate(flops=2 * 2 * n_req * n_tokens * slots * head_dim, bytes_accessed=8 * n_req * slots * head_dim, transcendentals=n_req * n_tokens * slots),
        name="attend",
    )(prefix, valid, queries, keys_new, values_new, k_cache, v_cache)


def mlp_partial(normed_full, w_gate, w_up, w_down):
    gate = jnp.einsum("rcd,df->rcf", normed_full, w_gate, preferred_element_type=jnp.float32)
    up_proj = jnp.einsum("rcd,df->rcf", normed_full, w_up, preferred_element_type=jnp.float32)
    hidden_act = (jax.nn.silu(gate) * up_proj).astype(jnp.bfloat16)
    return jnp.einsum("rcf,fd->rcd", hidden_act, w_down, preferred_element_type=jnp.float32).astype(jnp.bfloat16)


def rms_norm(hidden, gain):
    return scaled_norm(hidden.astype(jnp.float32), gain.astype(jnp.float32))


def add_rounded(first, second):
    return (first.astype(jnp.float32) + second.astype(jnp.float32)).astype(jnp.bfloat16)


def solution(mesh):
    row_spec = P("dp", "tp", None)
    cache_spec = P("dp", None, "tp", None)
    req_spec = P("dp")
    rep_spec = P(None)
    col_spec = P(None, "tp")
    bias_spec = P("tp")
    down_spec = P("tp", None)

    def layer(x_rows, k_cache, v_cache, prefix, valid, g_attn, w_q, b_q, w_k, b_k, w_v, b_v, w_o, g_mlp, w_gate, w_up, w_down):
        n_req, own_tokens, width = x_rows.shape
        w_all = jnp.concatenate([w_q, w_k, w_v], axis=1)
        bias_all = jnp.concatenate([b_q, b_k, b_v])
        queries, keys_new, values_new = project_all(x_rows, g_attn, w_all, bias_all, prefix)
        flat = (k_cache.shape[0], k_cache.shape[1], k_cache.shape[3])
        attended, k_out, v_out = attend(queries, keys_new, values_new, k_cache.reshape(flat), v_cache.reshape(flat), prefix, valid)
        attended = jnp.moveaxis(attended, 0, 1).reshape(n_req, 16 * own_tokens, flat[2])
        attn_part = jnp.einsum("rcn,nd->rcd", attended, w_o, preferred_element_type=jnp.float32).astype(jnp.bfloat16)
        attn_rows = lax.psum_scatter(attn_part, "tp", scatter_dimension=1, tiled=True)
        resid_mid = add_rounded(x_rows, attn_rows)
        normed_mlp = rms_norm(resid_mid, g_mlp)
        mlp_full = lax.all_gather(normed_mlp, "tp", axis=1, tiled=True)
        down_part = mlp_partial(mlp_full, w_gate, w_up, w_down)
        down_rows = lax.psum_scatter(down_part, "tp", scatter_dimension=1, tiled=True)
        return add_rounded(resid_mid, down_rows), k_out.reshape(k_cache.shape), v_out.reshape(v_cache.shape)

    in_specs = (row_spec, cache_spec, cache_spec, req_spec, req_spec, rep_spec, col_spec, bias_spec, col_spec, bias_spec, col_spec, bias_spec, down_spec, rep_spec, col_spec, col_spec, down_spec)
    return jax.shard_map(layer, mesh=mesh, in_specs=in_specs, out_specs=(row_spec, cache_spec, cache_spec), check_vma=False)
```

time: 753 us -> 535 us (0.71); the launches traced: 745 us -> 536 us
  Pallas kernels: 0 us -> 110 us
  waiting for transfers between devices: 466 us -> 364 us
  matrix products: 96.7 us -> 25 us
  local copies, waits for them, and re-layouts: 76.8 us -> 15.1 us
  other arithmetic: 59.8 us -> 8.16 us
  loops' own time: 30.8 us -> 0 us
    pallas_call x0 -> x2, Pallas kernels: none -> 110 us  [the longest x1 76 us: project_all(): pl.pallas_call(project_body, out_shape=(out, out, out), in_specs=[vmem] *...]
    all_gather x1 -> x0, waiting for transfers between devices: 103 us -> none  [layer(): normed_full = lax.all_gather(normed, 'tp', axis=1, tiled=True)]
    dot_general x5 -> x0, matrix products: 71.4 us -> none  [the longest x3 24.6 us: project(): jnp.einsum('rcd,dn->rcn', hidden, weight, preferred_element_type=jnp.floa...]
    another operation x2 -> x0, loops' own time: 30.8 us -> none  [write_rows(): return lax.fori_loop(0, cache.shape[0], body, cache)]
    dynamic_update_slice x16 -> x0, local copies, waits for them, and re-layouts: 27.3 us -> none  [body(): return lax.dynamic_update_slice(buffer, merged, (req_idx, start, 0, 0))]
    reduce_sum x3 -> x1, other arithmetic: 22.7 us -> 0.75 us  [scaled_norm(): jnp.mean(wide_vals * wide_vals, axis=-1, keepdims=True) + NORM_EPS]
    dynamic_slice x48 -> x0, local copies, waits for them, and re-layouts: 20.2 us -> none  [the longest x16 9.82 us: body(): start = prefix[req_idx]]
    select_n x16 -> x0, other arithmetic: 16.7 us -> none  [body(): merged = jnp.where(row_ids < valid[req_idx], fresh, old_rows)]
  transfers between devices with their start and end apart: 4 -> 3, of which waited for: 4 -> 3; matrix products, arithmetic and copies ran while one was open for 0% -> 0% of each run, Pallas kernels for 0% -> 0%
where the time goes in v1:
time: 535 us; the launch traced here: 536 us
  waiting for transfers between devices  364 us (68%)
  Pallas kernels  110 us (21%)
  matrix products  25 us (5%)
  local copies, waits for them, and re-layouts  15.1 us (3%)
  between operations  13.9 us (3%)
  other arithmetic  8.16 us (2%)
    unnamed x5, waiting for transfers between devices  264 us
    all_gather x1, waiting for transfers between devices, layer(): mlp_full = lax.all_gather(normed_mlp, 'tp', axis=1, tiled=True)  99.7 us
    pallas_call x1, Pallas kernels, project_all(): pl.pallas_call(project_body, out_shape=(out, out, out), in_specs=[vmem] *...  76 us
    pallas_call x1, Pallas kernels, attend(): pl.pallas_call(attention_body, out_shape=(jax.ShapeDtypeStruct(queries.sh...  33.6 us
    unnamed x24, local copies, waits for them, and re-layouts  14.3 us
  transfers between devices with their start and end apart: 3, of which 3 were waited for; matrix products, arithmetic and copies ran while one was open for 0% of the time, Pallas kernels for 0%

profile of v1, /device:TPU:0, one launch (start us, length us, event | category | flops | bytes accessed | tf_op | source)
XLA Modules:
  0.0 536.0 jit_solution(3473363952025642755)
XLA Ops:
  7.2 0.8 convert_element_type.38
  8.1 0.7 pad_maximum_fusion.1
  8.8 0.7 fusion.9
  9.6 0.1 multiply_sine_fusion
  9.7 0.7 broadcast_in_dim.4.gain_ref
  10.4 1.7 pad_maximum_fusion.w_ref
  12.2 76.0 %project.1 = (bf16[3072,128]{1,0:T(8,128)(2,1)S(1)}, bf16[3072,128]{1,0:T(8,128)(2,1)S(1)}, bf16[3072,128]{1,0:T(8,128)(2,1)S(1)}) custom-call(bf16[192,2048]{1,0:T(8,128)(2,1)S(1)} %bitcast.52, bf16[1,2048]{1,0:T(2,128)(2,1)S(1)} %broadcast_in_dim.4.gain_ref, bf16[2048,384]{1,0:T(8,128)(2,1)S(1)} %pad_maximum_fusion.w_ref, ...), custom_call_target="tpu_custom_call" | custom-call | flops 4831838208 | bytes 1572864 | tf_op jit(solution)/shard_map/project/pallas_call | solution.py:208
  88.2 33.6 %attend.1 = (bf16[16,8,24,128]{3,2,1,0:T(8,128)(2,1)S(1)}, bf16[8,4096,128]{2,1,0:T(8,128)(2,1)}, bf16[8,4096,128]{2,1,0:T(8,128)(2,1)}) custom-call(s32[8]{0:T(128)S(1)} %copy-done.2, s32[8]{0:T(128)S(1)} %copy-done.3, bf16[16,8,24,128]{3,2,1,0:T(8,128)(2,1)S(1)} %bitcast.57, bf16[16,8,24,128]{3,2,1,0:T(8,128)(2,1)S(1)} %bitcast.58, ...), custom_call_target="tpu_custom_call" | custom-call | flops 6442450944 | bytes 33554432 | tf_op jit(solution)/shard_map/attend/pallas_call | solution.py:298
  121.9 3.6 fusion.14
  125.5 5.1 copy.32
  130.7 0.6 copy-done.5
  131.3 132.1 %reduce-scatter.7.cloned.1.call-done = bf16[24,16384]{1,0:T(8,128)(2,1)} async-done(((bf16[384,16384]{1,0:T(8,128)(2,1)}), bf16[24,16384]{1,0:T(8,128)(2,1)}) %reduce-scatter.7.cloned.1.call-update) | async-done | bytes 786448
  263.4 1.6 copy.33
  265.0 0.7 fusion
  265.8 1.5 fusion.2
  267.3 0.2 reduce-scatter.9.cloned.1.call-start
  267.5 99.7 %all-gather.2.cloned.1.call-done = bf16[8,384,2048]{2,1,0:T(8,128)(2,1)} async-done(((bf16[8,24,2048]{2,1,0:T(8,128)(2,1)}), bf16[8,384,2048]{2,1,0:T(8,128)(2,1)}) %all-gather.2.cloned.1.call-update) | async-done | bytes 12582928 | tf_op jit(solution)/shard_map/all_gather | solution.py:355
  367.1 9.0 %fusion.5 = f32[8,384,344]{1,2,0:T(8,128)S(1)} fusion(bf16[8,384,2048]{2,1,0:T(8,128)(2,1)} %all-gather.2.cloned.1.call-done, bf16[2048,344]{0,1:T(8,128)(2,1)} %param.32), kind=kOutput, calls=%fused_computation.13 | convolution fusion | flops 4328521728 | bytes 18219008 | tf_op jit(solution)/shard_map/rcd,df->rcf/dot_general | solution.py:321
  376.2 5.4 %multiply_convert_fusion = bf16[8,384,344]{1,2,0:T(8,128)(2,1)S(1)} fusion(f32[8,384,344]{1,2,0:T(8,128)S(1)} %fusion.5, bf16[8,384,2048]{2,1,0:T(8,128)(2,1)S(1)} %copy-done.6, bf16[2048,344]{0,1:T(8,128)(2,1)S(1)} %copy-done.7), kind=kOutput, calls=%fused_computation.2 | convolution fusion | flops 4334862336 | bytes 20332544 | tf_op jit(solution)/shard_map/rcd,df->rcf/dot_general | solution.py:320
  381.5 7.1 %fusion.11 = bf16[48,8,8,2048]{3,1,0,2:T(8,128)(2,1)S(1)} fusion(bf16[8,384,344]{1,2,0:T(8,128)(2,1)S(1)} %multiply_convert_fusion, bf16[344,2048]{1,0:T(8,128)(2,1)S(1)} %copy-done), kind=kOutput, calls=%fused_computation.26 | convolution fusion | flops 4334813184 | bytes 16105472 | tf_op jit(solution)/shard_map/rcf,fd->rcd/dot_general | solution.py:323
  388.6 5.4 %copy.34 = bf16[48,8,8,2048]{3,1,2,0:T(8,128)(2,1)} copy(bf16[48,8,8,2048]{3,1,0,2:T(8,128)(2,1)S(1)} %fusion.11) | data formatting | bytes 25165824
  394.1 132.0 %reduce-scatter.9.cloned.1.call-done = bf16[24,16384]{1,0:T(8,128)(2,1)} async-done(((bf16[384,16384]{1,0:T(8,128)(2,1)}), bf16[24,16384]{1,0:T(8,128)(2,1)}) %reduce-scatter.9.cloned.1.call-update) | async-done | bytes 786448
  526.1 1.6 copy.35
  527.6 1.8 fusion.3
  (31 shorter events, 0.4 us)
Async XLA Ops:
  7.2 374.4 %copy-start = (bf16[344,2048]{1,0:T(8,128)(2,1)S(1)}, bf16[344,2048]{1,0:T(8,128)(2,1)}, u32[]{:S(2)}) copy-start(bf16[344,2048]{1,0:T(8,128)(2,1)} %param.33) | copy-start | bytes 4227076
  7.2 4.9 copy-start.1
  7.2 256.3 %reduce-scatter.7.cloned.1.call-start = ((), (), s32[]{:S(2)}) async-start(), calls=%async_computation.3 | async-start | bytes 13369344
  10.4 77.7 %slice-start = ((s8[8388608]{0:T(1024)(128)(4,1)}), s8[4194304]{0:T(1024)(128)(4,1)S(1)}, s32[]{:S(2)}) async-start(s8[8388608]{0:T(1024)(128)(4,1)} %bitcast.54), calls=%async_computation.5 | async-start | bytes 8388608
  12.1 76.0 %slice-start.1 = ((s8[8388608]{0:T(1024)(128)(4,1)}), s8[4194304]{0:T(1024)(128)(4,1)S(1)}, s32[]{:S(2)}) async-start(s8[8388608]{0:T(1024)(128)(4,1)} %bitcast.54), calls=%async_computation.6 | async-start | bytes 8388608
  12.1 76.0 %copy-start.2 = (s32[8]{0:T(128)S(1)}, s32[8]{0:T(128)}, u32[]{:S(2)}) copy-start(s32[8]{0:T(128)} %prefix_ref.1) | copy-start | bytes 100
  12.1 76.0 %copy-start.3 = (s32[8]{0:T(128)S(1)}, s32[8]{0:T(128)}, u32[]{:S(2)}) copy-start(s32[8]{0:T(128)} %valid_ref.1) | copy-start | bytes 100
  88.2 33.7 %copy-start.4 = (bf16[128,2048]{1,0:T(8,128)(2,1)S(1)}, bf16[128,2048]{1,0:T(8,128)(2,1)}, u32[]{:S(2)}) copy-start(bf16[128,2048]{1,0:T(8,128)(2,1)} %param.29) | copy-start | bytes 1572868
  130.6 0.7 copy-start.5
  130.7 236.5 %all-gather.2.cloned.1.call-start = ((), (), s32[]{:S(2)}) async-start(), calls=%async_computation.2 | async-start | bytes 13369344 | tf_op jit(solution)/shard_map/all_gather | solution.py:355
  267.3 258.8 %reduce-scatter.9.cloned.1.call-start = ((), (), s32[]{:S(2)}) async-start(), calls=%async_computation.4 | async-start | bytes 13369344
  367.1 9.0 %copy-start.6 = (bf16[8,384,2048]{2,1,0:T(8,128)(2,1)S(1)}, bf16[8,384,2048]{2,1,0:T(8,128)(2,1)}, u32[]{:S(2)}) copy-start(bf16[8,384,2048]{2,1,0:T(8,128)(2,1)} %all-gather.2.cloned.1.call-done) | copy-start | bytes 37748740
  367.1 9.0 %copy-start.7 = (bf16[2048,344]{0,1:T(8,128)(2,1)S(1)}, bf16[2048,344]{0,1:T(8,128)(2,1)}, u32[]{:S(2)}) copy-start(bf16[2048,344]{0,1:T(8,128)(2,1)} %param.31) | copy-start | bytes 4227076
Sparse Core Ops, SparseCore 0:
  130.8 132.6 reduce-scatter.6
  267.4 99.7 all-gather.1
  394.2 131.8 reduce-scatter.8

commit v2 on v1

--- a/solution.py
+++ b/solution.py
@@ -316,19 +316,185 @@
     )(prefix, valid, queries, keys_new, values_new, k_cache, v_cache)
 
 
-def mlp_partial(normed_full, w_gate, w_up, w_down):
-    gate = jnp.einsum("rcd,df->rcf", normed_full, w_gate, preferred_element_type=jnp.float32)
-    up_proj = jnp.einsum("rcd,df->rcf", normed_full, w_up, preferred_element_type=jnp.float32)
-    hidden_act = (jax.nn.silu(gate) * up_proj).astype(jnp.bfloat16)
-    return jnp.einsum("rcf,fd->rcd", hidden_act, w_down, preferred_element_type=jnp.float32).astype(jnp.bfloat16)
-
-
-def rms_norm(hidden, gain):
-    return scaled_norm(hidden.astype(jnp.float32), gain.astype(jnp.float32))
-
-
-def add_rounded(first, second):
-    return (first.astype(jnp.float32) + second.astype(jnp.float32)).astype(jnp.bfloat16)
+REDUCE = ((2, 3, 1, 0), (2, 3, 0, 1), (1, 0, 3, 2), (1, 0, 2, 3))
+COMPUTE = tuple((r[0], r[2], r[3], r[1]) for r in REDUCE)
+
+
+def finish_body(o_ref, x_ref, gain_ref, w_gate_ref, w_up_ref, w_down_ref, w_o_ref, out_ref,
+                rows_buf, part, attended, resid, acc, from_twin, from_line, from_lower, from_upper,
+                gather_send, gather_recv, reduce_send, twin_recv, line_recv, lower_recv, upper_recv, swap_send, swap_recv, local_sem):
+    where = place()
+    dp, z, y, c = where
+    rows, width = x_ref.shape
+    head_dim = o_ref.shape[1]
+    me = z * 4 + y * 2 + c
+    piece = rows // CHUNKS
+    load = pltpu.make_async_copy(w_o_ref, part.at[pl.ds(0, w_o_ref.shape[0])], local_sem)
+    load.start()
+    barrier = pltpu.get_barrier_semaphore()
+    for k in range(1, 16):
+        pl.semaphore_signal(barrier, 1, device_id=(dp, (me + k) % 16), device_id_type=MESH_ID)
+    pl.semaphore_wait(barrier, 15)
+
+    def block_rows(block):
+        return pl.ds(pl.multiple_of(block * rows, 16), rows)
+
+    mine = pl.ds(pl.multiple_of(me * head_dim, 128), head_dim)
+    for k in range(1, 16):
+        other = (me + k) % 16
+        pltpu.make_async_remote_copy(
+            src_ref=o_ref.at[block_rows(other)], dst_ref=attended.at[:, mine], send_sem=swap_send, recv_sem=swap_recv,
+            device_id=(dp, other), device_id_type=MESH_ID).start()
+    attended[:, mine] = o_ref[block_rows(me), :]
+    load.wait()
+    others = o_ref.at[pl.ds(0, 15 * rows)]
+    swap = pltpu.make_async_remote_copy(src_ref=others, dst_ref=others, send_sem=swap_send, recv_sem=swap_recv, device_id=(dp, 0), device_id_type=MESH_ID)
+    swap.wait_recv()
+    swap.wait_send()
+
+    @pl.loop(0, width // 256)
+    def _(n):
+        cols = pl.ds(pl.multiple_of(n * 256, 256), 256)
+        out = jnp.dot(attended[...], part[pl.ds(0, w_o_ref.shape[0]), cols], preferred_element_type=jnp.float32).astype(jnp.bfloat16)
+        resid[:, cols] = (x_ref[:, cols].astype(jnp.float32) + out.astype(jnp.float32)).astype(jnp.bfloat16)
+
+    rows_buf[block_rows(me), :] = scaled_norm(resid[...].astype(jnp.float32), gain_ref[...].astype(jnp.float32))
+    gather = RowGather(rows_buf, gather_send, gather_recv, where)
+    gather.early()
+
+    def partial_sums(block):
+        hidden = rows_buf[block_rows(block), :]
+        dims = (((1,), (1,)), ((), ()))
+        gate = lax.dot_general(hidden, w_gate_ref[...], dims, preferred_element_type=jnp.float32)
+        up = lax.dot_general(hidden, w_up_ref[...], dims, preferred_element_type=jnp.float32)
+        act = (jax.nn.silu(gate) * up).astype(jnp.bfloat16)
+        part[block_rows(block), :] = jnp.dot(act, w_down_ref[...], preferred_element_type=jnp.float32).astype(jnp.bfloat16)
+
+    def twin_copy(block, slot):
+        return pltpu.make_async_remote_copy(
+            src_ref=part.at[block_rows(block)], dst_ref=from_twin.at[block_rows(slot)], send_sem=reduce_send.at[TO_TWIN], recv_sem=twin_recv.at[slot],
+            device_id=(dp, z * 4 + y * 2 + 1 - c), device_id_type=MESH_ID)
+
+    def piece_copy(dest, line, j, way, buf, sems, device):
+        return pltpu.make_async_remote_copy(
+            src_ref=part.at[pl.ds(pl.multiple_of((dest * 4 + line * 2 + c) * rows + j * piece, 16), piece)],
+            dst_ref=buf.at[pl.ds(pl.multiple_of(dest * rows + j * piece, 16), piece)],
+            send_sem=reduce_send.at[way], recv_sem=sems.at[dest * CHUNKS + j], device_id=(dp, device), device_id_type=MESH_ID)
+
+    def line_send(dest):
+        for j in range(CHUNKS):
+            piece_copy(dest, 1 - y, j, TO_OTHER_LINE, from_line, line_recv, z * 4 + (1 - y) * 2 + c).start()
+
+    @pl.loop(0, 8)
+    def _(m):
+        is_own = (m >= 1) & (m <= 4)
+        at = jnp.where(is_own, chip_at(ARRIVAL, z, (m + 3) % 4), chip_at(COMPUTE, z, m % 4))
+        line = jnp.where(is_own, y, 1 - y)
+        pl.when(m == 7)(gather.late)
+        block = at * 4 + line * 2 + c
+        twin = at * 4 + line * 2 + 1 - c
+        gather.twin_arrived(twin)
+        partial_sums(twin)
+        twin_copy(twin, at * 2 + line).start()
+        partial_sums(block)
+        twin_copy(block, at * 2 + line).wait_recv()
+        total = part[block_rows(block), :].astype(jnp.float32) + from_twin[block_rows(at * 2 + line), :].astype(jnp.float32)
+        part[block_rows(block), :] = total.astype(jnp.bfloat16)
+
+        @pl.when((m == 0) | (m == 7))
+        def _():
+            line_send(at)
+
+    line_send(chip_at(REDUCE, z, 2))
+    line_send(chip_at(REDUCE, z, 3))
+
+    @pl.loop(0, LINE * CHUNKS)
+    def _(step):
+        dest = chip_at(REDUCE, z, step // CHUNKS)
+        j = step % CHUNKS
+        here = pl.ds(pl.multiple_of((dest * 4 + y * 2 + c) * rows + j * piece, 16), piece)
+        slot = pl.ds(pl.multiple_of(dest * rows + j * piece, 16), piece)
+        piece_copy(dest, y, j, TO_OTHER_LINE, from_line, line_recv, me).wait_recv()
+        acc[...] = part[here, :].astype(jnp.float32) + from_line[slot, :].astype(jnp.float32)
+
+        @pl.when((dest >= z) & (z > 0))
+        def _():
+            piece_copy(dest, y, j, TO_UPPER, from_lower, lower_recv, me).wait_recv()
+            acc[...] += from_lower[slot, :].astype(jnp.float32)
+
+        @pl.when((dest <= z) & (z < LINE - 1))
+        def _():
+            piece_copy(dest, y, j, TO_LOWER, from_upper, upper_recv, me).wait_recv()
+            acc[...] += from_upper[slot, :].astype(jnp.float32)
+
+        @pl.when(dest != z)
+        def _():
+            part[here, :] = acc[...].astype(jnp.bfloat16)
+
+        @pl.when(dest > z)
+        def _():
+            piece_copy(dest, y, j, TO_UPPER, from_lower, lower_recv, (z + 1) * 4 + y * 2 + c).start()
+
+        @pl.when(dest < z)
+        def _():
+            piece_copy(dest, y, j, TO_LOWER, from_upper, upper_recv, (z - 1) * 4 + y * 2 + c).start()
+
+        @pl.when(dest == z)
+        def _():
+            out = pl.ds(pl.multiple_of(j * piece, 16), piece)
+            down = acc[...].astype(jnp.bfloat16).astype(jnp.float32)
+            out_ref[out, :] = (resid[out, :].astype(jnp.float32) + down).astype(jnp.bfloat16)
+
+    gather.drain()
+
+    def sent(way, blocks):
+        span = pl.ds(0, blocks * rows)
+        pltpu.make_async_remote_copy(
+            src_ref=part.at[span], dst_ref=part.at[span], send_sem=reduce_send.at[way], recv_sem=twin_recv.at[0],
+            device_id=(dp, 0), device_id_type=MESH_ID).wait_send()
+
+    for zc in range(LINE):
+
+        @pl.when(z == zc)
+        def _(zc=zc):
+            if zc < LINE - 1:
+                sent(TO_UPPER, LINE - 1 - zc)
+            if zc > 0:
+                sent(TO_LOWER, zc)
+
+    sent(TO_OTHER_LINE, LINE)
+    sent(TO_TWIN, 2 * LINE)
+
+
+def finish(attended, x_rows, gain, w_gate, w_up, w_down, w_o):
+    n_req, own_tokens, width = x_rows.shape
+    rows = n_req * own_tokens
+    head_dim = attended.shape[-1]
+    vmem = pl.BlockSpec(memory_space=pltpu.VMEM)
+    bf16, f32 = jnp.bfloat16, jnp.float32
+    dma = pltpu.SemaphoreType.DMA
+    out = pl.pallas_call(
+        finish_body,
+        out_shape=jax.ShapeDtypeStruct((rows, width), bf16),
+        in_specs=[vmem] * 6 + [pl.BlockSpec(memory_space=pl.ANY)],
+        out_specs=vmem,
+        scratch_shapes=[
+            pltpu.VMEM((16 * rows, width), bf16),
+            pltpu.VMEM((16 * rows, width), bf16),
+            pltpu.VMEM((rows, width), bf16),
+            pltpu.VMEM((rows, width), bf16),
+            pltpu.VMEM((rows // CHUNKS, width), f32),
+            pltpu.VMEM((8 * rows, width), bf16),
+            pltpu.VMEM((4 * rows, width), bf16),
+            pltpu.VMEM((4 * rows, width), bf16),
+            pltpu.VMEM((4 * rows, width), bf16),
+            dma((4,)), dma((16 * CHUNKS,)), dma((4,)), dma((8,)), dma((4 * CHUNKS,)), dma((4 * CHUNKS,)), dma((4 * CHUNKS,)), dma, dma, dma,
+        ],
+        compiler_params=pltpu.CompilerParams(collective_id=1, has_side_effects=True, vmem_limit_bytes=62 * 2**20),
+        cost_estimate=pl.CostEstimate(flops=2 * rows * width * (width + 16 * 3 * w_down.shape[0]), bytes_accessed=4 * width * width, transcendentals=0),
+        name="finish",
+    )(attended.reshape(16 * rows, head_dim), x_rows.reshape(rows, width), gain[None, :], w_gate.T, w_up.T, w_down, w_o)
+    return out.reshape(x_rows.shape)
 
 
 def solution(mesh):
@@ -341,21 +507,14 @@
     down_spec = P("tp", None)
 
     def layer(x_rows, k_cache, v_cache, prefix, valid, g_attn, w_q, b_q, w_k, b_k, w_v, b_v, w_o, g_mlp, w_gate, w_up, w_down):
-        n_req, own_tokens, width = x_rows.shape
         w_all = jnp.concatenate([w_q, w_k, w_v], axis=1)
         bias_all = jnp.concatenate([b_q, b_k, b_v])
+        w_o_full = lax.all_gather(w_o, "tp", axis=0, tiled=True)
         queries, keys_new, values_new = project_all(x_rows, g_attn, w_all, bias_all, prefix)
         flat = (k_cache.shape[0], k_cache.shape[1], k_cache.shape[3])
         attended, k_out, v_out = attend(queries, keys_new, values_new, k_cache.reshape(flat), v_cache.reshape(flat), prefix, valid)
-        attended = jnp.moveaxis(attended, 0, 1).reshape(n_req, 16 * own_tokens, flat[2])
-        attn_part = jnp.einsum("rcn,nd->rcd", attended, w_o, preferred_element_type=jnp.float32).astype(jnp.bfloat16)
-        attn_rows = lax.psum_scatter(attn_part, "tp", scatter_dimension=1, tiled=True)
-        resid_mid = add_rounded(x_rows, attn_rows)
-        normed_mlp = rms_norm(resid_mid, g_mlp)
-        mlp_full = lax.all_gather(normed_mlp, "tp", axis=1, tiled=True)
-        down_part = mlp_partial(mlp_full, w_gate, w_up, w_down)
-        down_rows = lax.psum_scatter(down_part, "tp", scatter_dimension=1, tiled=True)
-        return add_rounded(resid_mid, down_rows), k_out.reshape(k_cache.shape), v_out.reshape(v_cache.shape)
+        x_out = finish(attended, x_rows, g_mlp, w_gate, w_up, w_down, w_o_full)
+        return x_out, k_out.reshape(k_cache.shape), v_out.reshape(v_cache.shape)
 
     in_specs = (row_spec, cache_spec, cache_spec, req_spec, req_spec, rep_spec, col_spec, bias_spec, col_spec, bias_spec, col_spec, bias_spec, down_spec, rep_spec, col_spec, col_spec, down_spec)
     return jax.shard_map(layer, mesh=mesh, in_specs=in_specs, out_specs=(row_spec, cache_spec, cache_spec), check_vma=False)

time: 535 us -> 344 us (0.64)
  waiting for transfers between devices: 364 us -> 0.68 us
  Pallas kernels: 110 us -> 317 us
  matrix products: 25 us -> 0 us
  local copies, waits for them, and re-layouts: 15.1 us -> 4.99 us
    unnamed x5 -> x1, waiting for transfers between devices: 264 us -> 0.68 us
    pallas_call x0 -> x1, Pallas kernels: none -> 172 us  [finish(): pl.pallas_call(finish_body, out_shape=jax.ShapeDtypeStruct((rows, width),...]
    all_gather x1, waiting for transfers between devices: 99.7 us -> 0.01 us  [layer(): w_o_full = lax.all_gather(w_o, 'tp', axis=0, tiled=True)]
    pallas_call x1, Pallas kernels: 76 us -> 114 us  [project_all(): pl.pallas_call(project_body, out_shape=(out, out, out), in_specs=[vmem] *...]
    dot_general x4 -> x0, matrix products: 25 us -> none  [the longest x1 8.99 us: mlp_partial(): jnp.einsum('rcd,df->rcf', normed_full, w_up, preferred_element_type=jnp.f...]
    unnamed x24 -> x13, local copies, waits for them, and re-layouts: 14.3 us -> 3 us
  transfers between devices with their start and end apart: 3 -> 1, of which waited for: 3 -> 0; matrix products, arithmetic and copies ran while one was open for 0% -> 2% of each run, Pallas kernels for 0% -> 42%
where the time goes in v2:
time: 344 us; the launch traced here: 341 us
  Pallas kernels  317 us (92%)
  between operations  14.1 us (4%)
  local copies, waits for them, and re-layouts  4.99 us (1%)
  other arithmetic  4.01 us (1%)
    pallas_call x1, Pallas kernels, finish(): pl.pallas_call(finish_body, out_shape=jax.ShapeDtypeStruct((rows, width),...  172 us
    pallas_call x1, Pallas kernels, project_all(): pl.pallas_call(project_body, out_shape=(out, out, out), in_specs=[vmem] *...  114 us
    pallas_call x1, Pallas kernels, attend(): pl.pallas_call(attention_body, out_shape=(jax.ShapeDtypeStruct(queries.sh...  30.3 us
  transfers between devices with their start and end apart: 1, of which 0 were waited for; matrix products, arithmetic and copies ran while one was open for 2% of the time, Pallas kernels for 42%

profile of v2, /device:TPU:0, one launch (start us, length us, event | category | flops | bytes accessed | tf_op | source)
XLA Modules:
  0.0 340.7 jit_solution(7271982986064876099)
XLA Ops:
  7.2 0.0 copy-start
  7.2 0.0 all-gather.2.cloned.1.call-start
  7.2 0.7 all-gather.2.cloned.1.call-update
  7.9 0.7 convert_element_type.3
  8.6 0.7 broadcast_in_dim.12.gain_ref
  9.3 0.7 pad_maximum_fusion.1
  10.0 1.3 broadcast_in_dim.14.gain_ref
  11.3 0.1 pad_maximum_fusion.2
  11.3 0.1 multiply_sine_fusion
  11.5 0.7 fusion
  12.2 0.0 slice-start
  12.2 1.7 pad_maximum_fusion.w_ref
  13.9 0.0 copy-done
  13.9 0.0 slice-start.1
  14.0 0.0 copy-start.1
  14.0 0.0 copy-start.2
  14.0 114.4 %project.1 = (bf16[3072,128]{1,0:T(8,128)(2,1)S(1)}, bf16[3072,128]{1,0:T(8,128)(2,1)S(1)}, bf16[3072,128]{1,0:T(8,128)(2,1)S(1)}) custom-call(bf16[192,2048]{1,0:T(8,128)(2,1)S(1)} %bitcast.20, bf16[1,2048]{1,0:T(2,128)(2,1)S(1)} %broadcast_in_dim.12.gain_ref, bf16[2048,384]{1,0:T(8,128)(2,1)S(1)} %pad_maximum_fusion.w_ref, ...), custom_call_target="tpu_custom_call" | custom-call | flops 4831838208 | bytes 1572864 | tf_op jit(solution)/shard_map/project/pallas_call | solution.py:208
  128.3 0.0 slice-done
  128.4 0.0 slice-done.1
  128.4 0.0 copy-done.1
  128.4 30.3 %attend.1 = (bf16[16,8,24,128]{3,2,1,0:T(8,128)(2,1)S(1)}, bf16[8,4096,128]{2,1,0:T(8,128)(2,1)}, bf16[8,4096,128]{2,1,0:T(8,128)(2,1)}) custom-call(s32[8]{0:T(128)S(1)} %copy-done.1, s32[8]{0:T(128)S(1)} %copy-done.2, bf16[16,8,24,128]{3,2,1,0:T(8,128)(2,1)S(1)} %bitcast.21, bf16[16,8,24,128]{3,2,1,0:T(8,128)(2,1)S(1)} %bitcast.22, ...), custom_call_target="tpu_custom_call" | custom-call | flops 6442450944 | bytes 33554432 | tf_op jit(solution)/shard_map/attend/pallas_call | solution.py:298
  158.7 0.9 copy-done.3
  159.6 172.2 %finish.1 = bf16[192,2048]{1,0:T(8,128)(2,1)} custom-call(bf16[3072,128]{1,0:T(8,128)(2,1)} %bitcast.24, bf16[192,2048]{1,0:T(8,128)(2,1)} %bitcast.19, bf16[1,2048]{1,0:T(2,128)(2,1)} %broadcast_in_dim.14.gain_ref, bf16[344,2048]{1,0:T(8,128)(2,1)} %bitcast.27, bf16[344,2048]{1,0:T(8,128)(2,1)} %bitcast.28, bf16[344,2048]{1,0:T(8,128)(2,1)} %w_down_ref.1, ...), custom_call_target="tpu_custom_call" | custom-call | flops 14596177920 | bytes 16777216 | tf_op jit(solution)/shard_map/finish/pallas_call | solution.py:476
  331.8 2.1 copy.23
  (6 shorter events, 0.0 us)
Async XLA Ops:
  7.2 6.8 %copy-start = (bf16[8,24,2048]{2,1,0:T(8,128)(2,1)S(1)}, bf16[8,24,2048]{2,1,0:T(8,128)(2,1)}, u32[]{:S(2)}) copy-start(bf16[8,24,2048]{2,1,0:T(8,128)(2,1)} %param.17) | copy-start | bytes 2359300
  7.2 152.4 %all-gather.2.cloned.1.call-start = ((), (), s32[]{:S(2)}) async-start(), calls=%async_computation | async-start | bytes 8912896 | tf_op jit(solution)/shard_map/all_gather | solution.py:512
  12.2 116.1 %slice-start = ((s8[8388608]{0:T(1024)(128)(4,1)}), s8[4194304]{0:T(1024)(128)(4,1)S(1)}, s32[]{:S(2)}) async-start(s8[8388608]{0:T(1024)(128)(4,1)} %bitcast.16), calls=%async_computation.1 | async-start | bytes 8388608
  13.9 114.4 %slice-start.1 = ((s8[8388608]{0:T(1024)(128)(4,1)}), s8[4194304]{0:T(1024)(128)(4,1)S(1)}, s32[]{:S(2)}) async-start(s8[8388608]{0:T(1024)(128)(4,1)} %bitcast.16), calls=%async_computation.2 | async-start | bytes 8388608
  14.0 114.4 %copy-start.1 = (s32[8]{0:T(128)S(1)}, s32[8]{0:T(128)}, u32[]{:S(2)}) copy-start(s32[8]{0:T(128)} %prefix_ref.1) | copy-start | bytes 100
  14.0 114.4 %copy-start.2 = (s32[8]{0:T(128)S(1)}, s32[8]{0:T(128)}, u32[]{:S(2)}) copy-start(s32[8]{0:T(128)} %valid_ref.1) | copy-start | bytes 100
  158.7 0.9 copy-start.3
Sparse Core Ops, SparseCore 0:
  10.1 112.4 all-gather.1

commit v3 on v2

--- a/solution.py
+++ b/solution.py
@@ -15,8 +15,9 @@
 
 MESH_ID = pl.DeviceIdType.MESH
 LINE = 4
-CHUNKS = 4
-TO_UPPER, TO_LOWER, TO_OTHER_LINE, TO_TWIN = range(4)
+CHUNKS = 6
+ALONG_FIRST = CHUNKS - 1
+TO_UPPER, TO_LOWER, TO_OTHER_LINE, TO_TWIN, TO_OTHER_GROUP = range(5)
 ARRIVAL = ((0, 1, 2, 3), (1, 0, 2, 3), (2, 1, 3, 0), (3, 2, 1, 0))
 
 
@@ -36,26 +37,32 @@
     return (code >> (2 * m)) & 3
 
 
-def greet(devices_of):
-    dp, z, y, c = devices_of
+def has(way, zc):
+    return zc < LINE - 1 if way == TO_UPPER else zc > 0
+
+
+def target(way, zc, y, c):
+    return {TO_UPPER: (zc + 1) * 4 + y * 2 + c, TO_LOWER: (zc - 1) * 4 + y * 2 + c, TO_OTHER_LINE: zc * 4 + (1 - y) * 2 + c, TO_TWIN: zc * 4 + y * 2 + 1 - c}[way]
+
+
+def greet(where):
+    dp, z, y, c = where
     barrier = pltpu.get_barrier_semaphore()
-
-    @pl.when(z > 0)
-    def _():
-        pl.semaphore_signal(barrier, 1, device_id=(dp, (z - 1) * 4 + y * 2 + c), device_id_type=MESH_ID)
-
-    @pl.when(z < LINE - 1)
-    def _():
-        pl.semaphore_signal(barrier, 1, device_id=(dp, (z + 1) * 4 + y * 2 + c), device_id_type=MESH_ID)
-
-    pl.semaphore_signal(barrier, 1, device_id=(dp, z * 4 + (1 - y) * 2 + c), device_id_type=MESH_ID)
-    pl.semaphore_signal(barrier, 1, device_id=(dp, z * 4 + y * 2 + 1 - c), device_id_type=MESH_ID)
-    pl.semaphore_wait(barrier, 2 + (z + 3) // 4 + (6 - z) // 4)
+    pl.when(z > 0)(lambda: pl.semaphore_signal(barrier, 1, device_id=(dp, target(TO_LOWER, z, y, c)), device_id_type=MESH_ID))
+    pl.when(z < LINE - 1)(lambda: pl.semaphore_signal(barrier, 1, device_id=(dp, target(TO_UPPER, z, y, c)), device_id_type=MESH_ID))
+    for way in (TO_OTHER_LINE, TO_TWIN):
+        pl.semaphore_signal(barrier, 1, device_id=(dp, target(way, z, y, c)), device_id_type=MESH_ID)
+    pl.semaphore_signal(barrier, 1, device_id=(1 - dp, z * 4 + y * 2 + c), device_id_type=MESH_ID)
+
+
+def meet(where):
+    dp, z, y, c = where
+    pl.semaphore_wait(pltpu.get_barrier_semaphore(), 3 + (z + 3) // 4 + (6 - z) // 4)
 
 
 class RowGather:
-    def __init__(self, buf, send_sem, recv_sem, where):
-        self.buf, self.send_sem, self.recv_sem = buf, send_sem, recv_sem
+    def __init__(self, buf, send_sem, recv_sem, where, weights=None):
+        self.buf, self.send_sem, self.recv_sem, self.weights = buf, send_sem, recv_sem, weights
         self.dp, self.z, self.y, self.c = where
         self.rows = buf.shape[0] // 16
         self.piece = self.rows // CHUNKS
@@ -74,56 +81,66 @@
     def arrived(self, block, j):
         self.copy(block, j, 0, 0).wait_recv()
 
-    def spread(self, block, j, zc, ups):
-        y, c = self.y, self.c
-        if ups[0] and zc < LINE - 1:
-            self.copy(block, j, TO_UPPER, (zc + 1) * 4 + y * 2 + c).start()
-        if ups[1] and zc > 0:
-            self.copy(block, j, TO_LOWER, (zc - 1) * 4 + y * 2 + c).start()
-        self.copy(block, j, TO_OTHER_LINE, zc * 4 + (1 - y) * 2 + c).start()
-        self.copy(block, j, TO_TWIN, zc * 4 + y * 2 + 1 - c).start()
-
-    def across(self, zc, m):
-        y, c = self.y, self.c
-        block = ARRIVAL[zc][m] * 4 + (1 - y) * 2 + c
-        for j in range(CHUNKS):
-            self.arrived(block, j)
-            self.copy(block, j, TO_TWIN, zc * 4 + y * 2 + 1 - c).start()
-
-    def early(self):
+    def spread(self, block, j, zc, ways):
+        for way in ways:
+            self.copy(block, j, way, target(way, zc, self.y, self.c)).start()
+
+    def line_block(self, zc, far, way_in):
+        at = zc - far if way_in == TO_UPPER else zc + far
+        return at * 4 + self.y * 2 + self.c, at * 4 + (1 - self.y) * 2 + self.c
+
+    def start(self):
         for zc in range(LINE):
 
             @pl.when(self.z == zc)
             def _(zc=zc):
-                y, c = self.y, self.c
-                for j in range(CHUNKS):
-                    self.spread(zc * 4 + y * 2 + c, j, zc, (True, True))
-                for far in range(1, LINE):
-                    for j in range(CHUNKS):
-                        if zc - far >= 0:
-                            block = (zc - far) * 4 + y * 2 + c
+                own, other = self.line_block(zc, 0, TO_UPPER)
+                along = tuple(way for way in (TO_UPPER, TO_LOWER) if has(way, zc))
+                self.spread(own, CHUNKS - 1, zc, (TO_OTHER_LINE,) + along + (TO_TWIN,))
+                for j in range(ALONG_FIRST):
+                    self.spread(own, j, zc, along + (TO_OTHER_LINE, TO_TWIN))
+                if self.weights is not None:
+                    self.weights.own(zc, along)
+                self.arrived(other, CHUNKS - 1)
+                self.spread(other, CHUNKS - 1, zc, along + (TO_TWIN,))
+
+    def across(self, zc, m):
+        block = ARRIVAL[zc][m] * 4 + (1 - self.y) * 2 + self.c
+        for j in range(ALONG_FIRST):
+            self.arrived(block, j)
+            self.spread(block, j, zc, (TO_TWIN,))
+        if self.weights is not None:
+            self.weights.pass_on(block, zc, ())
+
+    def step(self, s):
+        for far in range(1, LINE + 1):
+            for zc in range(LINE):
+
+                @pl.when((self.z == zc) & (s == far - 1))
+                def _(zc=zc, far=far):
+                    ways = [way for way in (TO_UPPER, TO_LOWER) if 0 <= (zc - far if way == TO_UPPER else zc + far) < LINE]
+                    for j in (CHUNKS - 1,) + tuple(range(ALONG_FIRST)):
+                        for way in ways:
+                            block = self.line_block(zc, far, way)[0]
+                            onward = (way,) if has(way, zc) else ()
                             self.arrived(block, j)
-                            self.spread(block, j, zc, (True, False))
-                        if zc + far < LINE:
-                            block = (zc + far) * 4 + y * 2 + c
-                            self.arrived(block, j)
-                            self.spread(block, j, zc, (False, True))
+                            self.spread(block, j, zc, onward + ((TO_OTHER_LINE,) if j < ALONG_FIRST else ()) + (TO_TWIN,))
+                    for way in ways:
+                        onward = (way,) if has(way, zc) else ()
+                        block, other = self.line_block(zc, far, way)
+                        if self.weights is not None:
+                            self.weights.pass_on(block, zc, onward + (TO_OTHER_LINE,))
+                        self.arrived(other, CHUNKS - 1)
+                        self.spread(other, CHUNKS - 1, zc, onward + (TO_TWIN,))
                     self.across(zc, far - 1)
-
-    def late(self):
-        for zc in range(LINE):
-
-            @pl.when(self.z == zc)
-            def _(zc=zc):
-                self.across(zc, LINE - 1)
 
     def twin_arrived(self, block):
         for j in range(CHUNKS):
             self.arrived(block, j)
 
     def drain(self):
-        def sent(way, blocks):
-            rows = pl.ds(0, blocks * self.rows)
+        def sent(way, pieces):
+            rows = pl.ds(0, pieces * self.piece)
             pltpu.make_async_remote_copy(
                 src_ref=self.buf.at[rows],
                 dst_ref=self.buf.at[rows],
@@ -138,15 +155,101 @@
             @pl.when(self.z == zc)
             def _(zc=zc):
                 if zc < LINE - 1:
+                    sent(TO_UPPER, (zc + 1) * (CHUNKS + 1))
+                if zc > 0:
+                    sent(TO_LOWER, (LINE - zc) * (CHUNKS + 1))
+
+        sent(TO_OTHER_LINE, LINE * ALONG_FIRST + 1)
+        sent(TO_TWIN, 2 * LINE * CHUNKS)
+
+
+class WeightGather:
+    def __init__(self, own_ref, full, send_sem, recv_sem, local_sem, where):
+        self.own_ref, self.full, self.send_sem, self.recv_sem, self.local_sem = own_ref, full, send_sem, recv_sem, local_sem
+        self.dp, self.z, self.y, self.c = where
+        self.half = own_ref.shape[0] // 2
+
+    def rows(self, block, half):
+        return pl.ds(pl.multiple_of((block * 2 + half) * self.half, 16), self.half)
+
+    def copy(self, src, block, half, way, device, group):
+        return pltpu.make_async_remote_copy(
+            src_ref=src,
+            dst_ref=self.full.at[self.rows(block, half)],
+            send_sem=self.send_sem.at[way],
+            recv_sem=self.recv_sem.at[block * 2 + half],
+            device_id=(group, device),
+            device_id_type=MESH_ID,
+        )
+
+    def keep(self):
+        block = self.z * 4 + self.y * 2 + self.c
+        rows = pl.ds(pl.multiple_of(block * 2 * self.half, 16), 2 * self.half)
+        return pltpu.make_async_copy(self.own_ref, self.full.at[rows], self.local_sem)
+
+    def own(self, zc, along):
+        block = zc * 4 + self.y * 2 + self.c
+        mine = self.own_ref.at[pl.ds(pl.multiple_of(self.dp * self.half, 16), self.half)]
+        for way in along + (TO_OTHER_LINE,):
+            self.copy(mine, block, self.dp, way, target(way, zc, self.y, self.c), self.dp).start()
+        for half in range(2):
+            src = self.own_ref.at[pl.ds(half * self.half, self.half)]
+            self.copy(src, block, half, TO_TWIN, target(TO_TWIN, zc, self.y, self.c), self.dp).start()
+
+    def pass_on(self, block, zc, ways):
+        held = self.full.at[self.rows(block, self.dp)]
+        self.copy(held, block, self.dp, 0, 0, self.dp).wait_recv()
+        for way in ways + (TO_TWIN,):
+            self.copy(held, block, self.dp, way, target(way, zc, self.y, self.c), self.dp).start()
+        me = zc * 4 + self.y * 2 + self.c
+        self.copy(held, block, self.dp, TO_OTHER_GROUP, me, 1 - self.dp).start()
+
+    def finish(self):
+        me = self.z * 4 + self.y * 2 + self.c
+        for k in range(1, 8):
+            block = (me + 2 * k) % 16
+            half = 1 - self.dp
+            held = self.full.at[self.rows(block, half)]
+            self.copy(held, block, half, 0, 0, self.dp).wait_recv()
+            self.copy(held, block, half, TO_TWIN, me + 1 - 2 * self.c, self.dp).start()
+        for k in range(8):
+            block = (me + 2 * k) % 16 + 1 - 2 * self.c
+            for half in range(2):
+                self.copy(self.full.at[self.rows(block, half)], block, half, 0, 0, self.dp).wait_recv()
+
+        def sent(way, halves):
+            rows = pl.ds(0, halves * self.half)
+            pltpu.make_async_remote_copy(
+                src_ref=self.full.at[rows], dst_ref=self.full.at[rows], send_sem=self.send_sem.at[way], recv_sem=self.recv_sem.at[0],
+                device_id=(self.dp, 0), device_id_type=MESH_ID).wait_send()
+
+        for zc in range(LINE):
+
+            @pl.when(self.z == zc)
+            def _(zc=zc):
+                if zc < LINE - 1:
                     sent(TO_UPPER, zc + 1)
                 if zc > 0:
                     sent(TO_LOWER, LINE - zc)
 
         sent(TO_OTHER_LINE, LINE)
-        sent(TO_TWIN, 2 * LINE)
-
-
-def project_body(x_ref, gain_ref, w_ref, bias_ref, base_cos_ref, base_sin_ref, step_cos_ref, step_sin_ref, q_ref, k_ref, v_ref, rows_buf, send_sem, recv_sem):
+        sent(TO_TWIN, 16)
+        sent(TO_OTHER_GROUP, 7)
+        self.keep().wait()
+
+
+def stage_chips(s):
+    return jnp.where(s == 0, 0, 2 * s + 1), jnp.where(s == LINE - 1, 8, 2 * s + 3)
+
+
+def chip_in_order(n, z, y):
+    own = (n < 2) | (n == 3) | (n == 5)
+    m = jnp.where(own, (n + 1) // 2, (n - 1) // 2)
+    return chip_at(ARRIVAL, z, m), jnp.where(own, y, 1 - y)
+
+
+def project_body(x_ref, gain_ref, wq_ref, wk_ref, wv_ref, bias_ref, base_cos_ref, base_sin_ref, step_cos_ref, step_sin_ref, w_o_ref,
+                 q_ref, k_ref, v_ref, w_o_full, rows_buf, w_buf, send_sem, recv_sem, w_send, w_recv, local_sem):
     where = place()
     dp, z, y, c = where
     rows = x_ref.shape[0]
@@ -154,14 +257,19 @@
     own_tokens = step_cos_ref.shape[0] // 16
     me = z * 4 + y * 2 + c
     own = pl.ds(pl.multiple_of(me * rows, 16), rows)
+    greet(where)
+    weights = WeightGather(w_o_ref, w_o_full, w_send, w_recv, local_sem, where)
+    weights.keep().start()
     rows_buf[own, :] = scaled_norm(x_ref[...].astype(jnp.float32), gain_ref[...].astype(jnp.float32))
-    greet(where)
-    gather = RowGather(rows_buf, send_sem, recv_sem, where)
-    gather.early()
+    meet(where)
+    gather = RowGather(rows_buf, send_sem, recv_sem, where, weights)
+    gather.start()
+    for i, ref in enumerate((wq_ref, wk_ref, wv_ref)):
+        w_buf[:, i * head_dim:(i + 1) * head_dim] = ref[...]
 
     def compute(block):
         at = pl.ds(pl.multiple_of(block * rows, 16), rows)
-        out = jnp.dot(rows_buf[at, :], w_ref[...], preferred_element_type=jnp.float32)
+        out = jnp.dot(rows_buf[at, :], w_buf[...], preferred_element_type=jnp.float32)
         out = (out + bias_ref[...].astype(jnp.float32)).astype(jnp.bfloat16)
         steps = pl.ds(pl.multiple_of(block * own_tokens, 8), own_tokens)
         step_cos, step_sin = step_cos_ref[steps, :][None], step_sin_ref[steps, :][None]
@@ -175,51 +283,50 @@
             ref[at, :] = (wide * cos_t + pltpu.roll(wide, head_dim // 2, 1) * sin_t).astype(jnp.bfloat16)
         v_ref[at, :] = out[:, 2 * head_dim:]
 
-    def chip(place_z, line):
-        compute(place_z * 4 + line * 2 + c)
-        twin = place_z * 4 + line * 2 + 1 - c
-        gather.twin_arrived(twin)
-        compute(twin)
-
-    @pl.loop(0, 6)
-    def _(m):
-        chip(chip_at(ARRIVAL, z, m % 4), (y + m // 4) % 2)
-
-    gather.late()
-
-    @pl.loop(2, 4)
-    def _(m):
-        chip(chip_at(ARRIVAL, z, m), 1 - y)
-
+    @pl.loop(0, LINE)
+    def _(s):
+        gather.step(s)
+
+        @pl.loop(*stage_chips(s))
+        def _(n):
+            at, line = chip_in_order(n, z, y)
+            compute(at * 4 + line * 2 + c)
+            twin = at * 4 + line * 2 + 1 - c
+            gather.twin_arrived(twin)
+            compute(twin)
+
+    weights.finish()
     gather.drain()
 
 
-def project_all(x_rows, gain, w_all, bias_all, prefix):
+def project_all(x_rows, gain, w_q, w_k, w_v, bias_all, w_o, prefix):
     n_req, own_tokens, width = x_rows.shape
     rows = n_req * own_tokens
-    head_dim = w_all.shape[1] // 3
+    head_dim = w_q.shape[1]
     half = head_dim // 2
     inv_freq = ROPE_THETA ** (-(jnp.arange(half, dtype=jnp.float32) * 2.0) / head_dim)
     inv_freq = jnp.concatenate([inv_freq, inv_freq])[None, :]
     base = prefix.astype(jnp.float32)[:, None] * inv_freq
     step = jnp.arange(16 * own_tokens, dtype=jnp.float32)[:, None] * inv_freq
     vmem = pl.BlockSpec(memory_space=pltpu.VMEM)
+    hbm = pl.BlockSpec(memory_space=pltpu.HBM)
     out = jax.ShapeDtypeStruct((16 * rows, head_dim), jnp.bfloat16)
-    outs = pl.pallas_call(
+    dma = pltpu.SemaphoreType.DMA
+    *outs, w_o_full = pl.pallas_call(
         project_body,
-        out_shape=(out, out, out),
-        in_specs=[vmem] * 8,
-        out_specs=(vmem,) * 3,
+        out_shape=(out, out, out, jax.ShapeDtypeStruct((16 * w_o.shape[0], w_o.shape[1]), jnp.bfloat16)),
+        in_specs=[vmem] * 11,
+        out_specs=(vmem,) * 3 + (hbm,),
         scratch_shapes=[
             pltpu.VMEM((16 * rows, width), jnp.bfloat16),
-            pltpu.SemaphoreType.DMA((4,)),
-            pltpu.SemaphoreType.DMA((16 * CHUNKS,)),
+            pltpu.VMEM((width, 3 * head_dim), jnp.bfloat16),
+            dma((4,)), dma((16 * CHUNKS,)), dma((5,)), dma((32,)), dma,
         ],
         compiler_params=pltpu.CompilerParams(collective_id=0, has_side_effects=True, vmem_limit_bytes=40 * 2**20),
         cost_estimate=pl.CostEstimate(flops=2 * 16 * rows * width * 3 * head_dim, bytes_accessed=4 * rows * width, transcendentals=0),
         name="project",
-    )(x_rows.reshape(rows, width), gain[None, :], w_all, bias_all[None, :], jnp.cos(base), jnp.sin(base), jnp.cos(step), jnp.sin(step))
-    return tuple(o.reshape(16, n_req, own_tokens, head_dim) for o in outs)
+    )(x_rows.reshape(rows, width), gain[None, :], w_q, w_k, w_v, bias_all[None, :], jnp.cos(base), jnp.sin(base), jnp.cos(step), jnp.sin(step), w_o)
+    return tuple(o.reshape(16, n_req, own_tokens, head_dim) for o in outs), w_o_full
 
 
 def token_rows(ref):
@@ -317,7 +424,6 @@
 
 
 REDUCE = ((2, 3, 1, 0), (2, 3, 0, 1), (1, 0, 3, 2), (1, 0, 2, 3))
-COMPUTE = tuple((r[0], r[2], r[3], r[1]) for r in REDUCE)
 
 
 def finish_body(o_ref, x_ref, gain_ref, w_gate_ref, w_up_ref, w_down_ref, w_o_ref, out_ref,
@@ -360,7 +466,7 @@
 
     rows_buf[block_rows(me), :] = scaled_norm(resid[...].astype(jnp.float32), gain_ref[...].astype(jnp.float32))
     gather = RowGather(rows_buf, gather_send, gather_recv, where)
-    gather.early()
+    gather.start()
 
     def partial_sums(block):
         hidden = rows_buf[block_rows(block), :]
@@ -375,80 +481,104 @@
             src_ref=part.at[block_rows(block)], dst_ref=from_twin.at[block_rows(slot)], send_sem=reduce_send.at[TO_TWIN], recv_sem=twin_recv.at[slot],
             device_id=(dp, z * 4 + y * 2 + 1 - c), device_id_type=MESH_ID)
 
-    def piece_copy(dest, line, j, way, buf, sems, device):
+    last = CHUNKS - 1
+
+    def piece_rows(block, j):
+        return pl.ds(pl.multiple_of(block * rows + j * piece, 16), piece)
+
+    def line_copy(dest, j):
         return pltpu.make_async_remote_copy(
-            src_ref=part.at[pl.ds(pl.multiple_of((dest * 4 + line * 2 + c) * rows + j * piece, 16), piece)],
-            dst_ref=buf.at[pl.ds(pl.multiple_of(dest * rows + j * piece, 16), piece)],
-            send_sem=reduce_send.at[way], recv_sem=sems.at[dest * CHUNKS + j], device_id=(dp, device), device_id_type=MESH_ID)
+            src_ref=part.at[piece_rows(dest * 4 + (1 - y) * 2 + c, j)], dst_ref=from_line.at[piece_rows(dest, j)],
+            send_sem=reduce_send.at[TO_OTHER_LINE], recv_sem=line_recv.at[dest * CHUNKS + j],
+            device_id=(dp, target(TO_OTHER_LINE, z, y, c)), device_id_type=MESH_ID)
+
+    def slot(dest, line, j):
+        far = jnp.where(line == y, dest * CHUNKS + j, LINE * CHUNKS + dest)
+        return far, pl.ds(pl.multiple_of(far * piece, 16), piece)
+
+    def along_copy(dest, line, j, way):
+        index, land = slot(dest, line, j)
+        buf, sems = (from_lower, lower_recv) if way == TO_UPPER else (from_upper, upper_recv)
+        return pltpu.make_async_remote_copy(
+            src_ref=part.at[piece_rows(dest * 4 + line * 2 + c, j)], dst_ref=buf.at[land],
+            send_sem=reduce_send.at[way], recv_sem=sems.at[index], device_id=(dp, target(way, z, y, c)), device_id_type=MESH_ID)
 
     def line_send(dest):
-        for j in range(CHUNKS):
-            piece_copy(dest, 1 - y, j, TO_OTHER_LINE, from_line, line_recv, z * 4 + (1 - y) * 2 + c).start()
-
-    @pl.loop(0, 8)
-    def _(m):
-        is_own = (m >= 1) & (m <= 4)
-        at = jnp.where(is_own, chip_at(ARRIVAL, z, (m + 3) % 4), chip_at(COMPUTE, z, m % 4))
-        line = jnp.where(is_own, y, 1 - y)
-        pl.when(m == 7)(gather.late)
-        block = at * 4 + line * 2 + c
-        twin = at * 4 + line * 2 + 1 - c
-        gather.twin_arrived(twin)
-        partial_sums(twin)
-        twin_copy(twin, at * 2 + line).start()
-        partial_sums(block)
-        twin_copy(block, at * 2 + line).wait_recv()
-        total = part[block_rows(block), :].astype(jnp.float32) + from_twin[block_rows(at * 2 + line), :].astype(jnp.float32)
-        part[block_rows(block), :] = total.astype(jnp.bfloat16)
-
-        @pl.when((m == 0) | (m == 7))
-        def _():
-            line_send(at)
-
-    line_send(chip_at(REDUCE, z, 2))
-    line_send(chip_at(REDUCE, z, 3))
-
-    @pl.loop(0, LINE * CHUNKS)
-    def _(step):
-        dest = chip_at(REDUCE, z, step // CHUNKS)
-        j = step % CHUNKS
-        here = pl.ds(pl.multiple_of((dest * 4 + y * 2 + c) * rows + j * piece, 16), piece)
-        slot = pl.ds(pl.multiple_of(dest * rows + j * piece, 16), piece)
-        piece_copy(dest, y, j, TO_OTHER_LINE, from_line, line_recv, me).wait_recv()
-        acc[...] = part[here, :].astype(jnp.float32) + from_line[slot, :].astype(jnp.float32)
+        for j in range(ALONG_FIRST):
+            line_copy(dest, j).start()
+
+    def chips(lo, hi):
+        @pl.loop(lo, hi)
+        def _(n):
+            at, line = chip_in_order(n, z, y)
+            block = at * 4 + line * 2 + c
+            twin = at * 4 + line * 2 + 1 - c
+            gather.twin_arrived(twin)
+            partial_sums(twin)
+            twin_copy(twin, at * 2 + line).start()
+            partial_sums(block)
+            twin_copy(block, at * 2 + line).wait_recv()
+            total = part[block_rows(block), :].astype(jnp.float32) + from_twin[block_rows(at * 2 + line), :].astype(jnp.float32)
+            part[block_rows(block), :] = total.astype(jnp.bfloat16)
+
+    @pl.loop(0, LINE)
+    def _(s):
+        gather.step(s)
+        pl.when(s == LINE - 1)(lambda: line_send(chip_at(REDUCE, z, 0)))
+        chips(*stage_chips(s))
+
+    for i in range(1, LINE):
+        line_send(chip_at(REDUCE, z, i))
+
+    def add_along(dest, line, j):
+        _, land = slot(dest, line, j)
 
         @pl.when((dest >= z) & (z > 0))
         def _():
-            piece_copy(dest, y, j, TO_UPPER, from_lower, lower_recv, me).wait_recv()
-            acc[...] += from_lower[slot, :].astype(jnp.float32)
+            along_copy(dest, line, j, TO_UPPER).wait_recv()
+            acc[...] += from_lower[land, :].astype(jnp.float32)
 
         @pl.when((dest <= z) & (z < LINE - 1))
         def _():
-            piece_copy(dest, y, j, TO_LOWER, from_upper, upper_recv, me).wait_recv()
-            acc[...] += from_upper[slot, :].astype(jnp.float32)
-
-        @pl.when(dest != z)
+            along_copy(dest, line, j, TO_LOWER).wait_recv()
+            acc[...] += from_upper[land, :].astype(jnp.float32)
+
+        @pl.when((dest != z) | (j == last))
         def _():
-            part[here, :] = acc[...].astype(jnp.bfloat16)
-
-        @pl.when(dest > z)
-        def _():
-            piece_copy(dest, y, j, TO_UPPER, from_lower, lower_recv, (z + 1) * 4 + y * 2 + c).start()
-
-        @pl.when(dest < z)
-        def _():
-            piece_copy(dest, y, j, TO_LOWER, from_upper, upper_recv, (z - 1) * 4 + y * 2 + c).start()
-
-        @pl.when(dest == z)
-        def _():
-            out = pl.ds(pl.multiple_of(j * piece, 16), piece)
-            down = acc[...].astype(jnp.bfloat16).astype(jnp.float32)
-            out_ref[out, :] = (resid[out, :].astype(jnp.float32) + down).astype(jnp.bfloat16)
-
+            part[piece_rows(dest * 4 + line * 2 + c, j), :] = acc[...].astype(jnp.bfloat16)
+
+        pl.when(dest > z)(lambda: along_copy(dest, line, j, TO_UPPER).start())
+        pl.when(dest < z)(lambda: along_copy(dest, line, j, TO_LOWER).start())
+
+    def result(j):
+        out = pl.ds(pl.multiple_of(j * piece, 16), piece)
+        down = acc[...].astype(jnp.bfloat16).astype(jnp.float32)
+        out_ref[out, :] = (resid[out, :].astype(jnp.float32) + down).astype(jnp.bfloat16)
+
+    @pl.loop(0, 2 * LINE)
+    def _(step):
+        dest = chip_at(REDUCE, z, step // 2)
+        line = (y + 1 + step) % 2
+        acc[...] = part[piece_rows(dest * 4 + line * 2 + c, last), :].astype(jnp.float32)
+        add_along(dest, line, last)
+        pl.when((dest == z) & (line != y))(lambda: line_copy(dest, last).start())
+
+    @pl.loop(0, LINE * ALONG_FIRST)
+    def _(step):
+        dest = chip_at(REDUCE, z, step // ALONG_FIRST)
+        j = step % ALONG_FIRST
+        line_copy(dest, j).wait_recv()
+        acc[...] = part[piece_rows(dest * 4 + y * 2 + c, j), :].astype(jnp.float32) + from_line[piece_rows(dest, j), :].astype(jnp.float32)
+        add_along(dest, y, j)
+        pl.when(dest == z)(lambda: result(j))
+
+    line_copy(z, last).wait_recv()
+    acc[...] = part[piece_rows(me, last), :].astype(jnp.float32) + from_line[piece_rows(z, last), :].astype(jnp.float32)
+    result(last)
     gather.drain()
 
-    def sent(way, blocks):
-        span = pl.ds(0, blocks * rows)
+    def sent(way, pieces):
+        span = pl.ds(0, pieces * piece)
         pltpu.make_async_remote_copy(
             src_ref=part.at[span], dst_ref=part.at[span], send_sem=reduce_send.at[way], recv_sem=twin_recv.at[0],
             device_id=(dp, 0), device_id_type=MESH_ID).wait_send()
@@ -458,12 +588,12 @@
         @pl.when(z == zc)
         def _(zc=zc):
             if zc < LINE - 1:
-                sent(TO_UPPER, LINE - 1 - zc)
+                sent(TO_UPPER, (LINE - 1 - zc) * (CHUNKS + 1))
             if zc > 0:
-                sent(TO_LOWER, zc)
-
-    sent(TO_OTHER_LINE, LINE)
-    sent(TO_TWIN, 2 * LINE)
+                sent(TO_LOWER, zc * (CHUNKS + 1))
+
+    sent(TO_OTHER_LINE, LINE * ALONG_FIRST + 1)
+    sent(TO_TWIN, 2 * LINE * CHUNKS)
 
 
 def finish(attended, x_rows, gain, w_gate, w_up, w_down, w_o):
@@ -476,7 +606,7 @@
     out = pl.pallas_call(
         finish_body,
         out_shape=jax.ShapeDtypeStruct((rows, width), bf16),
-        in_specs=[vmem] * 6 + [pl.BlockSpec(memory_space=pl.ANY)],
+        in_specs=[vmem] * 6 + [pl.BlockSpec(memory_space=pltpu.HBM)],
         out_specs=vmem,
         scratch_shapes=[
             pltpu.VMEM((16 * rows, width), bf16),
@@ -485,10 +615,10 @@
             pltpu.VMEM((rows, width), bf16),
             pltpu.VMEM((rows // CHUNKS, width), f32),
             pltpu.VMEM((8 * rows, width), bf16),
-            pltpu.VMEM((4 * rows, width), bf16),
-            pltpu.VMEM((4 * rows, width), bf16),
-            pltpu.VMEM((4 * rows, width), bf16),
-            dma((4,)), dma((16 * CHUNKS,)), dma((4,)), dma((8,)), dma((4 * CHUNKS,)), dma((4 * CHUNKS,)), dma((4 * CHUNKS,)), dma, dma, dma,
+            pltpu.VMEM((LINE * rows, width), bf16),
+            pltpu.VMEM((LINE * (rows + rows // CHUNKS), width), bf16),
+            pltpu.VMEM((LINE * (rows + rows // CHUNKS), width), bf16),
+            dma((4,)), dma((16 * CHUNKS,)), dma((4,)), dma((8,)), dma((LINE * CHUNKS,)), dma((LINE * (CHUNKS + 1),)), dma((LINE * (CHUNKS + 1),)), dma, dma, dma,
         ],
         compiler_params=pltpu.CompilerParams(collective_id=1, has_side_effects=True, vmem_limit_bytes=62 * 2**20),
         cost_estimate=pl.CostEstimate(flops=2 * rows * width * (width + 16 * 3 * w_down.shape[0]), bytes_accessed=4 * width * width, transcendentals=0),
@@ -507,10 +637,8 @@
     down_spec = P("tp", None)
 
     def layer(x_rows, k_cache, v_cache, prefix, valid, g_attn, w_q, b_q, w_k, b_k, w_v, b_v, w_o, g_mlp, w_gate, w_up, w_down):
-        w_all = jnp.concatenate([w_q, w_k, w_v], axis=1)
         bias_all = jnp.concatenate([b_q, b_k, b_v])
-        w_o_full = lax.all_gather(w_o, "tp", axis=0, tiled=True)
-        queries, keys_new, values_new = project_all(x_rows, g_attn, w_all, bias_all, prefix)
+        (queries, keys_new, values_new), w_o_full = project_all(x_rows, g_attn, w_q, w_k, w_v, bias_all, w_o, prefix)
         flat = (k_cache.shape[0], k_cache.shape[1], k_cache.shape[3])
         attended, k_out, v_out = attend(queries, keys_new, values_new, k_cache.reshape(flat), v_cache.reshape(flat), prefix, valid)
         x_out = finish(attended, x_rows, g_mlp, w_gate, w_up, w_down, w_o_full)

time: 344 us -> 313 us (0.910); the launches traced: 341 us -> 314 us
  Pallas kernels: 317 us -> 301 us
  between operations: 14.1 us -> 0.73 us
  local copies, waits for them, and re-layouts: 4.99 us -> 9.59 us
    pallas_call x1, Pallas kernels: 114 us -> 98.7 us  [project_all(): pl.pallas_call(project_body, out_shape=(out, out, out, jax.ShapeDtypeStru...]
    unnamed x13 -> x25, local copies, waits for them, and re-layouts: 3 us -> 8.28 us
  transfers between devices with their start and end apart: 1 -> 0, of which waited for: 0 -> 0; matrix products, arithmetic and copies ran while one was open for 2% -> 0% of each run, Pallas kernels for 42% -> 0%
where the time goes in v3:
time: 313 us; the launch traced here: 314 us
  Pallas kernels  301 us (96%)
  local copies, waits for them, and re-layouts  9.59 us (3%)
    pallas_call x1, Pallas kernels, finish(): pl.pallas_call(finish_body, out_shape=jax.ShapeDtypeStruct((rows, width),...  171 us
    pallas_call x1, Pallas kernels, project_all(): pl.pallas_call(project_body, out_shape=(out, out, out, jax.ShapeDtypeStru...  98.7 us
    pallas_call x1, Pallas kernels, attend(): pl.pallas_call(attention_body, out_shape=(jax.ShapeDtypeStruct(queries.sh...  31.1 us
    unnamed x25, local copies, waits for them, and re-layouts  8.28 us

profile of v3, /device:TPU:0, one launch (start us, length us, event | category | flops | bytes accessed | tf_op | source)
XLA Modules:
  0.0 314.2 jit_solution(5107734529837363915)
XLA Ops:
  0.6 0.1 pad_maximum_fusion.1
  0.7 0.7 fusion
  1.5 1.0 convert_element_type.3
  2.5 0.1 multiply_sine_fusion
  2.6 0.7 broadcast_in_dim.12.gain_ref
  3.3 0.7 pad_maximum_fusion
  4.0 1.1 copy-done
  5.1 1.0 copy-done.1
  6.2 1.0 copy-done.2
  7.2 1.0 copy-done.3
  8.3 1.0 copy-done.4
  9.3 98.7 %project.1 = (bf16[3072,128]{1,0:T(8,128)(2,1)S(1)}, bf16[3072,128]{1,0:T(8,128)(2,1)S(1)}, bf16[3072,128]{1,0:T(8,128)(2,1)S(1)}, bf16[2048,2048]{1,0:T(8,128)(2,1)S(1)}) custom-call(bf16[192,2048]{1,0:T(8,128)(2,1)S(1)} %bitcast.20, bf16[1,2048]{1,0:T(2,128)(2,1)S(1)} %broadcast_in_dim.12.gain_ref, bf16[2048,128]{1,0:T(8,128)(2,1)S(1)} %copy-done.1, ...), custom_call_target="tpu_custom_call" | custom-call | flops 4831838208 | bytes 1572864 | tf_op jit(solution)/shard_map/project/pallas_call | solution.py:315
  108.0 0.0 copy-start.8
  108.0 0.0 slice-done
  108.0 0.0 slice-done.1
  108.0 0.0 copy-done.5
  108.1 0.0 copy-done.6
  108.1 0.0 copy-start.9
  108.1 31.1 %attend.1 = (bf16[16,8,24,128]{3,2,1,0:T(8,128)(2,1)S(1)}, bf16[8,4096,128]{2,1,0:T(8,128)(2,1)}, bf16[8,4096,128]{2,1,0:T(8,128)(2,1)}) custom-call(s32[8]{0:T(128)S(1)} %copy-done.5, s32[8]{0:T(128)S(1)} %copy-done.6, bf16[16,8,24,128]{3,2,1,0:T(8,128)(2,1)S(1)} %bitcast.21, bf16[16,8,24,128]{3,2,1,0:T(8,128)(2,1)S(1)} %bitcast.22, ...), custom_call_target="tpu_custom_call" | custom-call | flops 6442450944 | bytes 33554432 | tf_op jit(solution)/shard_map/attend/pallas_call | solution.py:405
  139.2 0.0 copy-done.8
  139.2 0.9 copy-done.7
  140.1 0.6 broadcast_in_dim.14.gain_ref
  140.7 171.4 %finish.1 = bf16[192,2048]{1,0:T(8,128)(2,1)} custom-call(bf16[3072,128]{1,0:T(8,128)(2,1)} %bitcast.24, bf16[192,2048]{1,0:T(8,128)(2,1)} %bitcast.19, bf16[1,2048]{1,0:T(2,128)(2,1)} %broadcast_in_dim.14.gain_ref, bf16[344,2048]{1,0:T(8,128)(2,1)} %bitcast.27, bf16[344,2048]{1,0:T(8,128)(2,1)} %bitcast.28, bf16[344,2048]{1,0:T(8,128)(2,1)} %w_down_ref.1, ...), custom_call_target="tpu_custom_call" | custom-call | flops 14596177920 | bytes 16777216 | tf_op jit(solution)/shard_map/finish/pallas_call | solution.py:606
  312.1 2.1 copy.23
  (14 shorter events, 0.0 us)
Async XLA Ops:
  0.7 107.3 %slice-start = ((s8[8388608]{0:T(1024)(128)(4,1)}), s8[4194304]{0:T(1024)(128)(4,1)S(1)}, s32[]{:S(2)}) async-start(s8[8388608]{0:T(1024)(128)(4,1)} %bitcast.16), calls=%async_computation | async-start | bytes 8388608
  4.0 1.1 copy-start
  5.1 1.0 copy-start.1
  6.2 1.0 copy-start.2
  7.2 1.0 copy-start.3
  8.3 1.0 copy-start.4
  9.3 98.7 %slice-start.1 = ((s8[8388608]{0:T(1024)(128)(4,1)}), s8[4194304]{0:T(1024)(128)(4,1)S(1)}, s32[]{:S(2)}) async-start(s8[8388608]{0:T(1024)(128)(4,1)} %bitcast.16), calls=%async_computation.1 | async-start | bytes 8388608
  9.3 98.7 %copy-start.5 = (s32[8]{0:T(128)S(1)}, s32[8]{0:T(128)}, u32[]{:S(2)}) copy-start(s32[8]{0:T(128)} %prefix_ref.1) | copy-start | bytes 100
  9.3 98.7 %copy-start.6 = (s32[8]{0:T(128)S(1)}, s32[8]{0:T(128)}, u32[]{:S(2)}) copy-start(s32[8]{0:T(128)} %valid_ref.1) | copy-start | bytes 100
  108.0 31.2 %copy-start.8 = (bf16[2048,2048]{1,0:T(8,128)(2,1)}, bf16[2048,2048]{1,0:T(8,128)(2,1)S(1)}, u32[]{:S(2)}) copy-start(bf16[2048,2048]{1,0:T(8,128)(2,1)S(1)} %get-tuple-element.14.w_o_ref) | copy-start | bytes 25165828
  108.1 32.0 %copy-start.9 = (bf16[2048]{0:T(1024)(128)(2,1)S(1)}, bf16[2048]{0:T(1024)(128)(2,1)}, u32[]{:S(2)}) copy-start(bf16[2048]{0:T(1024)(128)(2,1)} %param.30) | copy-start | bytes 12292
  139.2 0.9 copy-start.7

commit v4 on v3

--- a/solution.py
+++ b/solution.py
@@ -1,6 +1,7 @@
 import functools
 import jax
 import jax.numpy as jnp
+import numpy as np
 from jax import lax
 from jax.experimental import pallas as pl
 from jax.experimental.pallas import tpu as pltpu
@@ -8,7 +9,7 @@
 
 ROPE_THETA = 1.0e6
 NORM_EPS = 1.0e-6
-KV_BLOCK = 512
+KV_BLOCK = 1024
 UPDATE_ROWS = 400
 LOG2_E = 1.4426950408889634
 
@@ -96,21 +97,21 @@
             def _(zc=zc):
                 own, other = self.line_block(zc, 0, TO_UPPER)
                 along = tuple(way for way in (TO_UPPER, TO_LOWER) if has(way, zc))
+                if self.weights is not None:
+                    self.weights.own(zc, along)
                 self.spread(own, CHUNKS - 1, zc, (TO_OTHER_LINE,) + along + (TO_TWIN,))
                 for j in range(ALONG_FIRST):
                     self.spread(own, j, zc, along + (TO_OTHER_LINE, TO_TWIN))
-                if self.weights is not None:
-                    self.weights.own(zc, along)
                 self.arrived(other, CHUNKS - 1)
                 self.spread(other, CHUNKS - 1, zc, along + (TO_TWIN,))
 
     def across(self, zc, m):
         block = ARRIVAL[zc][m] * 4 + (1 - self.y) * 2 + self.c
+        if self.weights is not None:
+            self.weights.pass_on(block, zc, ())
         for j in range(ALONG_FIRST):
             self.arrived(block, j)
             self.spread(block, j, zc, (TO_TWIN,))
-        if self.weights is not None:
-            self.weights.pass_on(block, zc, ())
 
     def step(self, s):
         for far in range(1, LINE + 1):
@@ -119,6 +120,9 @@
                 @pl.when((self.z == zc) & (s == far - 1))
                 def _(zc=zc, far=far):
                     ways = [way for way in (TO_UPPER, TO_LOWER) if 0 <= (zc - far if way == TO_UPPER else zc + far) < LINE]
+                    if self.weights is not None:
+                        for way in ways:
+                            self.weights.pass_on(self.line_block(zc, far, way)[0], zc, ((way,) if has(way, zc) else ()) + (TO_OTHER_LINE,))
                     for j in (CHUNKS - 1,) + tuple(range(ALONG_FIRST)):
                         for way in ways:
                             block = self.line_block(zc, far, way)[0]
@@ -128,8 +132,6 @@
                     for way in ways:
                         onward = (way,) if has(way, zc) else ()
                         block, other = self.line_block(zc, far, way)
-                        if self.weights is not None:
-                            self.weights.pass_on(block, zc, onward + (TO_OTHER_LINE,))
                         self.arrived(other, CHUNKS - 1)
                         self.spread(other, CHUNKS - 1, zc, onward + (TO_TWIN,))
                     self.across(zc, far - 1)
@@ -204,14 +206,20 @@
         me = zc * 4 + self.y * 2 + self.c
         self.copy(held, block, self.dp, TO_OTHER_GROUP, me, 1 - self.dp).start()
 
+    def swapped(self, place_z, line):
+        block, half = place_z * 4 + line * 2 + self.c, 1 - self.dp
+        held = self.full.at[self.rows(block, half)]
+        self.copy(held, block, half, 0, 0, self.dp).wait_recv()
+        self.copy(held, block, half, TO_TWIN, target(TO_TWIN, self.z, self.y, self.c), self.dp).start()
+
+    def swap_early(self):
+        for m in range(LINE - 1):
+            self.swapped(chip_at(ARRIVAL, self.z, m + 1), self.y)
+            self.swapped(chip_at(ARRIVAL, self.z, m), 1 - self.y)
+
     def finish(self):
         me = self.z * 4 + self.y * 2 + self.c
-        for k in range(1, 8):
-            block = (me + 2 * k) % 16
-            half = 1 - self.dp
-            held = self.full.at[self.rows(block, half)]
-            self.copy(held, block, half, 0, 0, self.dp).wait_recv()
-            self.copy(held, block, half, TO_TWIN, me + 1 - 2 * self.c, self.dp).start()
+        self.swapped(chip_at(ARRIVAL, self.z, LINE - 1), 1 - self.y)
         for k in range(8):
             block = (me + 2 * k) % 16 + 1 - 2 * self.c
             for half in range(2):
@@ -248,29 +256,34 @@
     return chip_at(ARRIVAL, z, m), jnp.where(own, y, 1 - y)
 
 
-def project_body(x_ref, gain_ref, wq_ref, wk_ref, wv_ref, bias_ref, base_cos_ref, base_sin_ref, step_cos_ref, step_sin_ref, w_o_ref,
-                 q_ref, k_ref, v_ref, w_o_full, rows_buf, w_buf, send_sem, recv_sem, w_send, w_recv, local_sem):
+def project_body(x_ref, gain_ref, wq_ref, wk_ref, wv_ref, bq_ref, bk_ref, bv_ref, base_cos_ref, base_sin_ref, step_cos_hbm, step_sin_hbm, w_o_ref,
+                 q_ref, k_ref, v_ref, w_o_full, rows_buf, w_buf, send_sem, recv_sem, w_send, w_recv, local_sem, load_sem, step_cos_ref, step_sin_ref):
     where = place()
     dp, z, y, c = where
     rows = x_ref.shape[0]
     head_dim = q_ref.shape[1]
     own_tokens = step_cos_ref.shape[0] // 16
     me = z * 4 + y * 2 + c
+    loads = [pltpu.make_async_copy(ref, w_buf.at[:, pl.ds(i * head_dim, head_dim)], load_sem.at[i]) for i, ref in enumerate((wq_ref, wk_ref, wv_ref))]
+    loads += [pltpu.make_async_copy(step_cos_hbm, step_cos_ref, load_sem.at[3]), pltpu.make_async_copy(step_sin_hbm, step_sin_ref, load_sem.at[4])]
     own = pl.ds(pl.multiple_of(me * rows, 16), rows)
     greet(where)
     weights = WeightGather(w_o_ref, w_o_full, w_send, w_recv, local_sem, where)
     weights.keep().start()
+    for load in loads:
+        load.start()
     rows_buf[own, :] = scaled_norm(x_ref[...].astype(jnp.float32), gain_ref[...].astype(jnp.float32))
     meet(where)
     gather = RowGather(rows_buf, send_sem, recv_sem, where, weights)
     gather.start()
-    for i, ref in enumerate((wq_ref, wk_ref, wv_ref)):
-        w_buf[:, i * head_dim:(i + 1) * head_dim] = ref[...]
+    for load in loads:
+        load.wait()
 
     def compute(block):
         at = pl.ds(pl.multiple_of(block * rows, 16), rows)
         out = jnp.dot(rows_buf[at, :], w_buf[...], preferred_element_type=jnp.float32)
-        out = (out + bias_ref[...].astype(jnp.float32)).astype(jnp.bfloat16)
+        bias = jnp.concatenate([ref[...].astype(jnp.float32) for ref in (bq_ref, bk_ref, bv_ref)], axis=1)
+        out = (out + bias).astype(jnp.bfloat16)
         steps = pl.ds(pl.multiple_of(block * own_tokens, 8), own_tokens)
         step_cos, step_sin = step_cos_ref[steps, :][None], step_sin_ref[steps, :][None]
         base_cos, base_sin = base_cos_ref[...][:, None, :], base_sin_ref[...][:, None, :]
@@ -286,6 +299,7 @@
     @pl.loop(0, LINE)
     def _(s):
         gather.step(s)
+        pl.when(s == LINE - 1)(weights.swap_early)
 
         @pl.loop(*stage_chips(s))
         def _(n):
@@ -299,15 +313,20 @@
     gather.drain()
 
 
-def project_all(x_rows, gain, w_q, w_k, w_v, bias_all, w_o, prefix):
+def inverse_frequencies(head_dim):
+    steps = np.arange(head_dim // 2, dtype=np.float32) * np.float32(2.0) / np.float32(head_dim)
+    half = np.power(np.float32(ROPE_THETA), -steps).astype(np.float32)
+    return np.concatenate([half, half])[None, :]
+
+
+def project_all(x_rows, gain, w_q, w_k, w_v, biases, w_o, prefix):
     n_req, own_tokens, width = x_rows.shape
     rows = n_req * own_tokens
     head_dim = w_q.shape[1]
-    half = head_dim // 2
-    inv_freq = ROPE_THETA ** (-(jnp.arange(half, dtype=jnp.float32) * 2.0) / head_dim)
-    inv_freq = jnp.concatenate([inv_freq, inv_freq])[None, :]
+    inv_freq = jnp.asarray(inverse_frequencies(head_dim))
     base = prefix.astype(jnp.float32)[:, None] * inv_freq
-    step = jnp.arange(16 * own_tokens, dtype=jnp.float32)[:, None] * inv_freq
+    step = np.arange(16 * own_tokens, dtype=np.float32)[:, None] * inverse_frequencies(head_dim)
+    step_cos, step_sin = np.cos(step), np.sin(step)
     vmem = pl.BlockSpec(memory_space=pltpu.VMEM)
     hbm = pl.BlockSpec(memory_space=pltpu.HBM)
     out = jax.ShapeDtypeStruct((16 * rows, head_dim), jnp.bfloat16)
@@ -315,17 +334,18 @@
     *outs, w_o_full = pl.pallas_call(
         project_body,
         out_shape=(out, out, out, jax.ShapeDtypeStruct((16 * w_o.shape[0], w_o.shape[1]), jnp.bfloat16)),
-        in_specs=[vmem] * 11,
+        in_specs=[vmem] * 2 + [hbm] * 3 + [vmem] * 5 + [hbm] * 2 + [vmem],
         out_specs=(vmem,) * 3 + (hbm,),
         scratch_shapes=[
             pltpu.VMEM((16 * rows, width), jnp.bfloat16),
             pltpu.VMEM((width, 3 * head_dim), jnp.bfloat16),
-            dma((4,)), dma((16 * CHUNKS,)), dma((5,)), dma((32,)), dma,
+            dma((4,)), dma((16 * CHUNKS,)), dma((5,)), dma((32,)), dma, dma((5,)),
+            pltpu.VMEM(step_cos.shape, jnp.float32), pltpu.VMEM(step_sin.shape, jnp.float32),
         ],
-        compiler_params=pltpu.CompilerParams(collective_id=0, has_side_effects=True, vmem_limit_bytes=40 * 2**20),
+        compiler_params=pltpu.CompilerParams(collective_id=0, has_side_effects=True, vmem_limit_bytes=62 * 2**20),
         cost_estimate=pl.CostEstimate(flops=2 * 16 * rows * width * 3 * head_dim, bytes_accessed=4 * rows * width, transcendentals=0),
         name="project",
-    )(x_rows.reshape(rows, width), gain[None, :], w_q, w_k, w_v, bias_all[None, :], jnp.cos(base), jnp.sin(base), jnp.cos(step), jnp.sin(step), w_o)
+    )(x_rows.reshape(rows, width), gain.reshape(1, width), w_q, w_k, w_v, *biases, jnp.cos(base), jnp.sin(base), step_cos, step_sin, w_o)
     return tuple(o.reshape(16, n_req, own_tokens, head_dim) for o in outs), w_o_full
 
 
@@ -417,7 +437,7 @@
                 pltpu.VMEM((n_tokens, head_dim), jnp.float32),
             ],
         ),
-        compiler_params=pltpu.CompilerParams(dimension_semantics=("arbitrary",), vmem_limit_bytes=40 * 2**20),
+        compiler_params=pltpu.CompilerParams(dimension_semantics=("arbitrary",), vmem_limit_bytes=62 * 2**20),
         cost_estimate=pl.CostEstimate(flops=2 * 2 * n_req * n_tokens * slots * head_dim, bytes_accessed=8 * n_req * slots * head_dim, transcendentals=n_req * n_tokens * slots),
         name="attend",
     )(prefix, valid, queries, keys_new, values_new, k_cache, v_cache)
@@ -426,17 +446,21 @@
 REDUCE = ((2, 3, 1, 0), (2, 3, 0, 1), (1, 0, 3, 2), (1, 0, 2, 3))
 
 
-def finish_body(o_ref, x_ref, gain_ref, w_gate_ref, w_up_ref, w_down_ref, w_o_ref, out_ref,
-                rows_buf, part, attended, resid, acc, from_twin, from_line, from_lower, from_upper,
-                gather_send, gather_recv, reduce_send, twin_recv, line_recv, lower_recv, upper_recv, swap_send, swap_recv, local_sem):
+def finish_body(o_ref, x_ref, gain_ref, w_gate_hbm, w_up_hbm, w_down_hbm, w_o_ref, out_ref,
+                rows_buf, part, swapped, attended, resid, acc, from_twin, from_line, from_lower, from_upper,
+                gather_send, gather_recv, reduce_send, twin_recv, line_recv, lower_recv, upper_recv, swap_send, swap_recv, local_sem, w_gate_ref, w_up_ref, w_down_ref):
     where = place()
     dp, z, y, c = where
     rows, width = x_ref.shape
     head_dim = o_ref.shape[1]
     me = z * 4 + y * 2 + c
     piece = rows // CHUNKS
-    load = pltpu.make_async_copy(w_o_ref, part.at[pl.ds(0, w_o_ref.shape[0])], local_sem)
+    load = pltpu.make_async_copy(w_o_ref, part.at[pl.ds(0, w_o_ref.shape[0])], local_sem.at[0])
     load.start()
+    pairs = ((w_gate_hbm, w_gate_ref), (w_up_hbm, w_up_ref), (w_down_hbm, w_down_ref))
+    mlp_loads = [pltpu.make_async_copy(src, dst, local_sem.at[1 + i]) for i, (src, dst) in enumerate(pairs)]
+    for mlp_load in mlp_loads:
+        mlp_load.start()
     barrier = pltpu.get_barrier_semaphore()
     for k in range(1, 16):
         pl.semaphore_signal(barrier, 1, device_id=(dp, (me + k) % 16), device_id_type=MESH_ID)
@@ -445,28 +469,31 @@
     def block_rows(block):
         return pl.ds(pl.multiple_of(block * rows, 16), rows)
 
-    mine = pl.ds(pl.multiple_of(me * head_dim, 128), head_dim)
     for k in range(1, 16):
         other = (me + k) % 16
         pltpu.make_async_remote_copy(
-            src_ref=o_ref.at[block_rows(other)], dst_ref=attended.at[:, mine], send_sem=swap_send, recv_sem=swap_recv,
+            src_ref=o_ref.at[block_rows(other)], dst_ref=swapped.at[block_rows(me)], send_sem=swap_send, recv_sem=swap_recv,
             device_id=(dp, other), device_id_type=MESH_ID).start()
-    attended[:, mine] = o_ref[block_rows(me), :]
+    swapped[block_rows(me), :] = o_ref[block_rows(me), :]
     load.wait()
     others = o_ref.at[pl.ds(0, 15 * rows)]
     swap = pltpu.make_async_remote_copy(src_ref=others, dst_ref=others, send_sem=swap_send, recv_sem=swap_recv, device_id=(dp, 0), device_id_type=MESH_ID)
     swap.wait_recv()
     swap.wait_send()
-
-    @pl.loop(0, width // 256)
+    for head in range(16):
+        attended[:, head * head_dim:(head + 1) * head_dim] = swapped[head * rows:(head + 1) * rows, :]
+
+    @pl.loop(0, width // 512)
     def _(n):
-        cols = pl.ds(pl.multiple_of(n * 256, 256), 256)
+        cols = pl.ds(pl.multiple_of(n * 512, 512), 512)
         out = jnp.dot(attended[...], part[pl.ds(0, w_o_ref.shape[0]), cols], preferred_element_type=jnp.float32).astype(jnp.bfloat16)
         resid[:, cols] = (x_ref[:, cols].astype(jnp.float32) + out.astype(jnp.float32)).astype(jnp.bfloat16)
 
     rows_buf[block_rows(me), :] = scaled_norm(resid[...].astype(jnp.float32), gain_ref[...].astype(jnp.float32))
     gather = RowGather(rows_buf, gather_send, gather_recv, where)
     gather.start()
+    for mlp_load in mlp_loads:
+        mlp_load.wait()
 
     def partial_sums(block):
         hidden = rows_buf[block_rows(block), :]
@@ -521,15 +548,6 @@
             total = part[block_rows(block), :].astype(jnp.float32) + from_twin[block_rows(at * 2 + line), :].astype(jnp.float32)
             part[block_rows(block), :] = total.astype(jnp.bfloat16)
 
-    @pl.loop(0, LINE)
-    def _(s):
-        gather.step(s)
-        pl.when(s == LINE - 1)(lambda: line_send(chip_at(REDUCE, z, 0)))
-        chips(*stage_chips(s))
-
-    for i in range(1, LINE):
-        line_send(chip_at(REDUCE, z, i))
-
     def add_along(dest, line, j):
         _, land = slot(dest, line, j)
 
@@ -555,22 +573,54 @@
         down = acc[...].astype(jnp.bfloat16).astype(jnp.float32)
         out_ref[out, :] = (resid[out, :].astype(jnp.float32) + down).astype(jnp.bfloat16)
 
-    @pl.loop(0, 2 * LINE)
-    def _(step):
+    at_end = (z == 0) | (z == LINE - 1)
+
+    def last_piece(step):
         dest = chip_at(REDUCE, z, step // 2)
         line = (y + 1 + step) % 2
         acc[...] = part[piece_rows(dest * 4 + line * 2 + c, last), :].astype(jnp.float32)
         add_along(dest, line, last)
         pl.when((dest == z) & (line != y))(lambda: line_copy(dest, last).start())
 
-    @pl.loop(0, LINE * ALONG_FIRST)
+    def before_last():
+        line_send(chip_at(REDUCE, z, 0))
+
+        @pl.when(at_end)
+        def _():
+            last_piece(0)
+            last_piece(1)
+            last_piece(3)
+
+    @pl.loop(0, LINE)
+    def _(s):
+        pl.when(s == LINE - 1)(before_last)
+        gather.step(s)
+        chips(*stage_chips(s))
+
+    for i in range(1, LINE):
+        line_send(chip_at(REDUCE, z, i))
+
+    @pl.loop(0, 2 * LINE - 2)
     def _(step):
-        dest = chip_at(REDUCE, z, step // ALONG_FIRST)
-        j = step % ALONG_FIRST
-        line_copy(dest, j).wait_recv()
-        acc[...] = part[piece_rows(dest * 4 + y * 2 + c, j), :].astype(jnp.float32) + from_line[piece_rows(dest, j), :].astype(jnp.float32)
-        add_along(dest, y, j)
-        pl.when(dest == z)(lambda: result(j))
+        pl.when(jnp.logical_not(at_end) | (step == 2) | (step >= 4))(lambda: last_piece(step))
+
+    @pl.loop(0, LINE * ALONG_FIRST + 2)
+    def _(n):
+        swing = (LINE - 1) * ALONG_FIRST
+
+        @pl.when((n >= swing) & (n < swing + 2))
+        def _():
+            last_piece(2 * LINE - 2 + n - swing)
+
+        @pl.when((n < swing) | (n >= swing + 2))
+        def _():
+            step = jnp.where(n < swing, n, n - 2)
+            dest = chip_at(REDUCE, z, step // ALONG_FIRST)
+            j = step % ALONG_FIRST
+            line_copy(dest, j).wait_recv()
+            acc[...] = part[piece_rows(dest * 4 + y * 2 + c, j), :].astype(jnp.float32) + from_line[piece_rows(dest, j), :].astype(jnp.float32)
+            add_along(dest, y, j)
+            pl.when(dest == z)(lambda: result(j))
 
     line_copy(z, last).wait_recv()
     acc[...] = part[piece_rows(me, last), :].astype(jnp.float32) + from_line[piece_rows(z, last), :].astype(jnp.float32)
@@ -606,11 +656,12 @@
     out = pl.pallas_call(
         finish_body,
         out_shape=jax.ShapeDtypeStruct((rows, width), bf16),
-        in_specs=[vmem] * 6 + [pl.BlockSpec(memory_space=pltpu.HBM)],
+        in_specs=[vmem] * 3 + [pl.BlockSpec(memory_space=pltpu.HBM)] * 4,
         out_specs=vmem,
         scratch_shapes=[
             pltpu.VMEM((16 * rows, width), bf16),
             pltpu.VMEM((16 * rows, width), bf16),
+            pltpu.VMEM((16 * rows, head_dim), bf16),
             pltpu.VMEM((rows, width), bf16),
             pltpu.VMEM((rows, width), bf16),
             pltpu.VMEM((rows // CHUNKS, width), f32),
@@ -618,7 +669,8 @@
             pltpu.VMEM((LINE * rows, width), bf16),
             pltpu.VMEM((LINE * (rows + rows // CHUNKS), width), bf16),
             pltpu.VMEM((LINE * (rows + rows // CHUNKS), width), bf16),
-            dma((4,)), dma((16 * CHUNKS,)), dma((4,)), dma((8,)), dma((LINE * CHUNKS,)), dma((LINE * (CHUNKS + 1),)), dma((LINE * (CHUNKS + 1),)), dma, dma, dma,
+            dma((4,)), dma((16 * CHUNKS,)), dma((4,)), dma((8,)), dma((LINE * CHUNKS,)), dma((LINE * (CHUNKS + 1),)), dma((LINE * (CHUNKS + 1),)), dma, dma, dma((4,)),
+            pltpu.VMEM(w_gate.T.shape, bf16), pltpu.VMEM(w_up.T.shape, bf16), pltpu.VMEM(w_down.shape, bf16),
         ],
         compiler_params=pltpu.CompilerParams(collective_id=1, has_side_effects=True, vmem_limit_bytes=62 * 2**20),
         cost_estimate=pl.CostEstimate(flops=2 * rows * width * (width + 16 * 3 * w_down.shape[0]), bytes_accessed=4 * width * width, transcendentals=0),
@@ -637,8 +689,8 @@
     down_spec = P("tp", None)
 
     def layer(x_rows, k_cache, v_cache, prefix, valid, g_attn, w_q, b_q, w_k, b_k, w_v, b_v, w_o, g_mlp, w_gate, w_up, w_down):
-        bias_all = jnp.concatenate([b_q, b_k, b_v])
-        (queries, keys_new, values_new), w_o_full = project_all(x_rows, g_attn, w_q, w_k, w_v, bias_all, w_o, prefix)
+        biases = [b.reshape(1, -1) for b in (b_q, b_k, b_v)]
+        (queries, keys_new, values_new), w_o_full = project_all(x_rows, g_attn, w_q, w_k, w_v, biases, w_o, prefix)
         flat = (k_cache.shape[0], k_cache.shape[1], k_cache.shape[3])
         attended, k_out, v_out = attend(queries, keys_new, values_new, k_cache.reshape(flat), v_cache.reshape(flat), prefix, valid)
         x_out = finish(attended, x_rows, g_mlp, w_gate, w_up, w_down, w_o_full)

time: 313 us -> 291 us (0.930)
  Pallas kernels: 301 us -> 283 us
  local copies, waits for them, and re-layouts: 9.59 us -> 3.99 us
    pallas_call x1, Pallas kernels: 171 us -> 158 us  [finish(): pl.pallas_call(finish_body, out_shape=jax.ShapeDtypeStruct((rows, width),...]
    unnamed x25 -> x3, local copies, waits for them, and re-layouts: 8.28 us -> 2.1 us
    pallas_call x1, Pallas kernels: 31.1 us -> 26.6 us  [attend(): pl.pallas_call(attention_body, out_shape=(jax.ShapeDtypeStruct(queries.sh...]
where the time goes in v4:
time: 291 us; the launch traced here: 290 us
  Pallas kernels  283 us (97%)
  local copies, waits for them, and re-layouts  3.99 us (1%)
    pallas_call x1, Pallas kernels, finish(): pl.pallas_call(finish_body, out_shape=jax.ShapeDtypeStruct((rows, width),...  158 us
    pallas_call x1, Pallas kernels, project_all(): pl.pallas_call(project_body, out_shape=(out, out, out, jax.ShapeDtypeStru...  98.8 us
    pallas_call x1, Pallas kernels, attend(): pl.pallas_call(attention_body, out_shape=(jax.ShapeDtypeStruct(queries.sh...  26.6 us

profile of v4, /device:TPU:0, one launch (start us, length us, event | category | flops | bytes accessed | tf_op | source)
XLA Modules:
  0.0 290.2 jit_solution(4813010427677898016)
XLA Ops:
  0.6 0.7 convert_element_type.3
  1.3 1.4 multiply_sine_fusion
  2.7 1.3 reshape.51.gain_ref
  3.9 98.8 %project.1 = (bf16[3072,128]{1,0:T(8,128)(2,1)}, bf16[3072,128]{1,0:T(8,128)(2,1)}, bf16[3072,128]{1,0:T(8,128)(2,1)}, bf16[2048,2048]{1,0:T(8,128)(2,1)}) custom-call(bf16[192,2048]{1,0:T(8,128)(2,1)} %bitcast.24, bf16[1,2048]{1,0:T(2,128)(2,1)} %reshape.51.gain_ref, bf16[2048,128]{1,0:T(8,128)(2,1)} %wq_ref.1, bf16[2048,128]{1,0:T(8,128)(2,1)} %wk_ref.1, ...), custom_call_target="tpu_custom_call" | custom-call | flops 4831838208 | bytes 1572864 | tf_op jit(solution)/shard_map/project/pallas_call | solution.py:334
  102.7 0.0 copy-start
  102.7 26.6 %attend.1 = (bf16[16,8,24,128]{3,2,1,0:T(8,128)(2,1)}, bf16[8,4096,128]{2,1,0:T(8,128)(2,1)}, bf16[8,4096,128]{2,1,0:T(8,128)(2,1)}) custom-call(s32[8]{0:T(128)} %prefix_ref.1, s32[8]{0:T(128)} %valid_ref.1, bf16[16,8,24,128]{3,2,1,0:T(8,128)(2,1)} %bitcast.31, bf16[16,8,24,128]{3,2,1,0:T(8,128)(2,1)} %bitcast.32, bf16[16,8,24,128]{3,2,1,0:T(8,128)(2,1)} %bitcast.33, ...), custom_call_target="tpu_custom_call" | custom-call | flops 6442450944 | bytes 33554432 | tf_op jit(solution)/shard_map/attend/pallas_call | solution.py:425
  129.3 0.0 copy-done
  129.3 0.6 broadcast_in_dim.4.gain_ref
  129.9 158.2 %finish.1 = bf16[192,2048]{1,0:T(8,128)(2,1)} custom-call(bf16[3072,128]{1,0:T(8,128)(2,1)} %bitcast.34, bf16[192,2048]{1,0:T(8,128)(2,1)} %bitcast.25, bf16[1,2048]{1,0:T(2,128)(2,1)} %broadcast_in_dim.4.gain_ref, bf16[344,2048]{1,0:T(8,128)(2,1)} %bitcast.22, bf16[344,2048]{1,0:T(8,128)(2,1)} %bitcast.23, bf16[344,2048]{1,0:T(8,128)(2,1)} %w_down_hbm.1, ...), custom_call_target="tpu_custom_call" | custom-call | flops 14596177920 | bytes 16777216 | tf_op jit(solution)/shard_map/finish/pallas_call | solution.py:656
  288.1 2.1 copy.26
Async XLA Ops:
  102.7 26.6 %copy-start = (bf16[2048]{0:T(1024)(128)(2,1)S(1)}, bf16[2048]{0:T(1024)(128)(2,1)}, u32[]{:S(2)}) copy-start(bf16[2048]{0:T(1024)(128)(2,1)} %param.33) | copy-start | bytes 12292

commit v5 on v4

--- a/solution.py
+++ b/solution.py
@@ -256,8 +256,8 @@
     return chip_at(ARRIVAL, z, m), jnp.where(own, y, 1 - y)
 
 
-def project_body(x_ref, gain_ref, wq_ref, wk_ref, wv_ref, bq_ref, bk_ref, bv_ref, base_cos_ref, base_sin_ref, step_cos_hbm, step_sin_hbm, w_o_ref,
-                 q_ref, k_ref, v_ref, w_o_full, rows_buf, w_buf, send_sem, recv_sem, w_send, w_recv, local_sem, load_sem, step_cos_ref, step_sin_ref):
+def project_body(x_ref, gain_ref, wq_ref, wk_ref, wv_ref, bq_ref, bk_ref, bv_ref, prefix_ref, coarse_cos_ref, coarse_sin_ref, step_cos_hbm, step_sin_hbm, w_o_ref,
+                 q_ref, k_ref, v_ref, w_o_full, rows_buf, w_buf, send_sem, recv_sem, w_send, w_recv, local_sem, load_sem, step_cos_ref, step_sin_ref, base_cos_ref, base_sin_ref):
     where = place()
     dp, z, y, c = where
     rows = x_ref.shape[0]
@@ -278,6 +278,12 @@
     gather.start()
     for load in loads:
         load.wait()
+    for r in range(base_cos_ref.shape[0]):
+        first = prefix_ref[r]
+        high, low = pl.ds(first // step_cos_ref.shape[0], 1), pl.ds(first % step_cos_ref.shape[0], 1)
+        coarse_cos, coarse_sin, fine_cos, fine_sin = coarse_cos_ref[high, :], coarse_sin_ref[high, :], step_cos_ref[low, :], step_sin_ref[low, :]
+        base_cos_ref[r:r + 1, :] = coarse_cos * fine_cos - coarse_sin * fine_sin
+        base_sin_ref[r:r + 1, :] = coarse_sin * fine_cos + coarse_cos * fine_sin
 
     def compute(block):
         at = pl.ds(pl.multiple_of(block * rows, 16), rows)
@@ -314,19 +320,19 @@
 
 
 def inverse_frequencies(head_dim):
-    steps = np.arange(head_dim // 2, dtype=np.float32) * np.float32(2.0) / np.float32(head_dim)
-    half = np.power(np.float32(ROPE_THETA), -steps).astype(np.float32)
+    half = ROPE_THETA ** (-2.0 * np.arange(head_dim // 2) / head_dim)
     return np.concatenate([half, half])[None, :]
 
 
-def project_all(x_rows, gain, w_q, w_k, w_v, biases, w_o, prefix):
+def project_all(x_rows, gain, w_q, w_k, w_v, biases, w_o, prefix, k_slots):
     n_req, own_tokens, width = x_rows.shape
     rows = n_req * own_tokens
     head_dim = w_q.shape[1]
-    inv_freq = jnp.asarray(inverse_frequencies(head_dim))
-    base = prefix.astype(jnp.float32)[:, None] * inv_freq
-    step = np.arange(16 * own_tokens, dtype=np.float32)[:, None] * inverse_frequencies(head_dim)
-    step_cos, step_sin = np.cos(step), np.sin(step)
+    inv_freq = inverse_frequencies(head_dim)
+    n_tokens = 16 * own_tokens
+    step = np.arange(n_tokens)[:, None] * inv_freq
+    coarse = np.arange(-(-k_slots // n_tokens))[:, None] * n_tokens * inv_freq
+    step_cos, step_sin, coarse_cos, coarse_sin = (np.asarray(t, np.float32) for t in (np.cos(step), np.sin(step), np.cos(coarse), np.sin(coarse)))
     vmem = pl.BlockSpec(memory_space=pltpu.VMEM)
     hbm = pl.BlockSpec(memory_space=pltpu.HBM)
     out = jax.ShapeDtypeStruct((16 * rows, head_dim), jnp.bfloat16)
@@ -334,18 +340,19 @@
     *outs, w_o_full = pl.pallas_call(
         project_body,
         out_shape=(out, out, out, jax.ShapeDtypeStruct((16 * w_o.shape[0], w_o.shape[1]), jnp.bfloat16)),
-        in_specs=[vmem] * 2 + [hbm] * 3 + [vmem] * 5 + [hbm] * 2 + [vmem],
+        in_specs=[vmem] * 2 + [hbm] * 3 + [vmem] * 3 + [pl.BlockSpec(memory_space=pltpu.SMEM)] + [vmem] * 2 + [hbm] * 2 + [vmem],
         out_specs=(vmem,) * 3 + (hbm,),
         scratch_shapes=[
             pltpu.VMEM((16 * rows, width), jnp.bfloat16),
             pltpu.VMEM((width, 3 * head_dim), jnp.bfloat16),
             dma((4,)), dma((16 * CHUNKS,)), dma((5,)), dma((32,)), dma, dma((5,)),
             pltpu.VMEM(step_cos.shape, jnp.float32), pltpu.VMEM(step_sin.shape, jnp.float32),
+            pltpu.VMEM((n_req, head_dim), jnp.float32), pltpu.VMEM((n_req, head_dim), jnp.float32),
         ],
         compiler_params=pltpu.CompilerParams(collective_id=0, has_side_effects=True, vmem_limit_bytes=62 * 2**20),
         cost_estimate=pl.CostEstimate(flops=2 * 16 * rows * width * 3 * head_dim, bytes_accessed=4 * rows * width, transcendentals=0),
         name="project",
-    )(x_rows.reshape(rows, width), gain.reshape(1, width), w_q, w_k, w_v, *biases, jnp.cos(base), jnp.sin(base), step_cos, step_sin, w_o)
+    )(x_rows.reshape(rows, width), gain.reshape(1, width), w_q, w_k, w_v, *biases, prefix, coarse_cos, coarse_sin, step_cos, step_sin, w_o)
     return tuple(o.reshape(16, n_req, own_tokens, head_dim) for o in outs), w_o_full
 
 
@@ -354,25 +361,45 @@
     return rows.reshape(rows.shape[0] * rows.shape[1], rows.shape[2])
 
 
-def attention_body(prefix_ref, valid_ref, q_ref, kn_ref, vn_ref, k_ref, v_ref, o_ref, ko_ref, vo_ref, scores, top, total, acc):
+def attention_body(prefix_ref, valid_ref, q_ref, kn_ref, vn_ref, k_ref, v_ref, o_ref, ko_ref, vo_ref, scores, top, total, acc, staged, take_sem, put_sem):
     req = pl.program_id(0)
     start = prefix_ref[req]
     count = valid_ref[req]
     head_dim = q_ref.shape[3]
     n_tokens = q_ref.shape[0] * q_ref.shape[2]
     slots = k_ref.shape[1]
-    ko_ref[...] = k_ref[...]
-    vo_ref[...] = v_ref[...]
+    last = pl.num_programs(0) - 1
+
+    def take(r):
+        return [pltpu.make_async_copy(ref.at[r], staged.at[r * 2 + i], take_sem.at[r * 2 + i]) for i, ref in enumerate((k_ref, v_ref))]
+
+    def put(r):
+        return [pltpu.make_async_copy(staged.at[r * 2 + i], ref.at[r], put_sem.at[r * 2 + i]) for i, ref in enumerate((ko_ref, vo_ref))]
+
+    @pl.when(req == 0)
+    def _():
+        for move in take(0) + take(1):
+            move.start()
+
+    @pl.when(req + 2 <= last)
+    def _():
+        for move in take(req + 2):
+            move.start()
+
+    for move in take(req):
+        move.wait()
     base = pl.multiple_of(jnp.minimum((start // 16) * 16, slots - UPDATE_ROWS), 16)
     shift = start - base
     row = lax.broadcasted_iota(jnp.int32, (UPDATE_ROWS, head_dim), 0) - shift
     keep = (row >= 0) & (row < count)
-    for src, dst in ((kn_ref, ko_ref), (vn_ref, vo_ref)):
+    for i, src in enumerate((kn_ref, vn_ref)):
         fresh = jnp.concatenate([token_rows(src), jnp.zeros((UPDATE_ROWS - n_tokens, head_dim), jnp.float32)], axis=0)
         fresh = pltpu.roll(fresh, shift, 0)
-        old = dst[0, pl.ds(base, UPDATE_ROWS), :].astype(jnp.float32)
-        dst[0, pl.ds(base, UPDATE_ROWS), :] = jnp.where(keep, fresh, old).astype(jnp.bfloat16)
-
+        old = staged[req * 2 + i, pl.ds(base, UPDATE_ROWS), :].astype(jnp.float32)
+        staged[req * 2 + i, pl.ds(base, UPDATE_ROWS), :] = jnp.where(keep, fresh, old).astype(jnp.bfloat16)
+
+    for move in put(req):
+        move.start()
     n_open = (start + 1) // KV_BLOCK
     n_used = pl.cdiv(start + count, KV_BLOCK)
     queries = token_rows(q_ref).astype(jnp.bfloat16)
@@ -380,7 +407,7 @@
     top[...] = jnp.full_like(top, -1.0e30)
 
     def score(blk, masked):
-        keys = ko_ref[0, pl.ds(pl.multiple_of(blk * KV_BLOCK, KV_BLOCK), KV_BLOCK), :]
+        keys = staged[req * 2, pl.ds(pl.multiple_of(blk * KV_BLOCK, KV_BLOCK), KV_BLOCK), :]
         s = lax.dot_general(queries, keys, (((1,), (1,)), ((), ())), preferred_element_type=jnp.float32)
         if masked:
             col = lax.broadcasted_iota(jnp.int32, (n_tokens, KV_BLOCK), 1) + blk * KV_BLOCK
@@ -408,11 +435,17 @@
             part = part + e
             pieces.append(e.astype(jnp.bfloat16))
         total[...] = part
-        vals = vo_ref[0, pl.ds(pl.multiple_of(blk * KV_BLOCK, KV_BLOCK), KV_BLOCK), :]
+        vals = staged[req * 2 + 1, pl.ds(pl.multiple_of(blk * KV_BLOCK, KV_BLOCK), KV_BLOCK), :]
         acc[...] += jnp.dot(jnp.concatenate(pieces, axis=1), vals, preferred_element_type=jnp.float32)
 
     mixed = acc[...] / jnp.sum(total[...], axis=1, keepdims=True)
     o_ref[:, 0] = mixed.reshape(o_ref.shape[0], o_ref.shape[2], head_dim).astype(jnp.bfloat16)
+
+    @pl.when(req == last)
+    def _():
+        for r in range(k_ref.shape[0]):
+            for move in put(r):
+                move.wait()
 
 
 def attend(queries, keys_new, values_new, k_cache, v_cache, prefix, valid):
@@ -420,7 +453,7 @@
     n_tokens = owners * own_tokens
     slots = k_cache.shape[1]
     new_spec = pl.BlockSpec((owners, 1, own_tokens, head_dim), lambda r, *_: (0, r, 0, 0))
-    cache_spec = pl.BlockSpec((1, slots, head_dim), lambda r, *_: (r, 0, 0))
+    cache_spec = pl.BlockSpec(memory_space=pltpu.HBM)
     cache_out = jax.ShapeDtypeStruct(k_cache.shape, jnp.bfloat16)
     return pl.pallas_call(
         attention_body,
@@ -435,6 +468,9 @@
                 pltpu.VMEM((n_tokens, 128), jnp.float32),
                 pltpu.VMEM((n_tokens, 128), jnp.float32),
                 pltpu.VMEM((n_tokens, head_dim), jnp.float32),
+                pltpu.VMEM((2 * n_req, slots, head_dim), jnp.bfloat16),
+                pltpu.SemaphoreType.DMA((2 * n_req,)),
+                pltpu.SemaphoreType.DMA((2 * n_req,)),
             ],
         ),
         compiler_params=pltpu.CompilerParams(dimension_semantics=("arbitrary",), vmem_limit_bytes=62 * 2**20),
@@ -690,7 +726,7 @@
 
     def layer(x_rows, k_cache, v_cache, prefix, valid, g_attn, w_q, b_q, w_k, b_k, w_v, b_v, w_o, g_mlp, w_gate, w_up, w_down):
         biases = [b.reshape(1, -1) for b in (b_q, b_k, b_v)]
-        (queries, keys_new, values_new), w_o_full = project_all(x_rows, g_attn, w_q, w_k, w_v, biases, w_o, prefix)
+        (queries, keys_new, values_new), w_o_full = project_all(x_rows, g_attn, w_q, w_k, w_v, biases, w_o, prefix, k_cache.shape[1])
         flat = (k_cache.shape[0], k_cache.shape[1], k_cache.shape[3])
         attended, k_out, v_out = attend(queries, keys_new, values_new, k_cache.reshape(flat), v_cache.reshape(flat), prefix, valid)
         x_out = finish(attended, x_rows, g_mlp, w_gate, w_up, w_down, w_o_full)

time: 291 us -> 289 us (level)
  Pallas kernels: 283 us -> 286 us
where the time goes in v5:
time: 289 us; the launch traced here: 291 us
  Pallas kernels  286 us (99%)
  local copies, waits for them, and re-layouts  4 us (1%)
    pallas_call x1, Pallas kernels, finish(): pl.pallas_call(finish_body, out_shape=jax.ShapeDtypeStruct((rows, width),...  158 us
    pallas_call x1, Pallas kernels, project_all(): pl.pallas_call(project_body, out_shape=(out, out, out, jax.ShapeDtypeStru...  98.8 us
    pallas_call x1, Pallas kernels, attend(): pl.pallas_call(attention_body, out_shape=(jax.ShapeDtypeStruct(queries.sh...  28.9 us

profile of v5, /device:TPU:0, one launch (start us, length us, event | category | flops | bytes accessed | tf_op | source)
XLA Modules:
  0.0 290.5 jit_solution(9982873789661717009)
XLA Ops:
  0.6 1.3 reshape.50.gain_ref
  1.9 98.8 %project.1 = (bf16[3072,128]{1,0:T(8,128)(2,1)}, bf16[3072,128]{1,0:T(8,128)(2,1)}, bf16[3072,128]{1,0:T(8,128)(2,1)}, bf16[2048,2048]{1,0:T(8,128)(2,1)}) custom-call(bf16[192,2048]{1,0:T(8,128)(2,1)} %bitcast.24, bf16[1,2048]{1,0:T(2,128)(2,1)} %reshape.50.gain_ref, bf16[2048,128]{1,0:T(8,128)(2,1)} %wq_ref.1, bf16[2048,128]{1,0:T(8,128)(2,1)} %wk_ref.1, ...), custom_call_target="tpu_custom_call" | custom-call | flops 4831838208 | bytes 1572864 | tf_op jit(solution)/shard_map/project/pallas_call | solution.py:340
  100.7 0.0 copy-start
  100.7 28.9 %attend.1 = (bf16[16,8,24,128]{3,2,1,0:T(8,128)(2,1)}, bf16[8,4096,128]{2,1,0:T(8,128)(2,1)}, bf16[8,4096,128]{2,1,0:T(8,128)(2,1)}) custom-call(s32[8]{0:T(128)} %prefix_ref.3, s32[8]{0:T(128)} %valid_ref.1, bf16[16,8,24,128]{3,2,1,0:T(8,128)(2,1)} %bitcast.31, bf16[16,8,24,128]{3,2,1,0:T(8,128)(2,1)} %bitcast.32, bf16[16,8,24,128]{3,2,1,0:T(8,128)(2,1)} %bitcast.33, ...), custom_call_target="tpu_custom_call" | custom-call | flops 6442450944 | bytes 33554432 | tf_op jit(solution)/shard_map/attend/pallas_call | solution.py:458
  129.7 0.0 copy-done
  129.7 0.6 broadcast_in_dim.3.gain_ref
  130.3 158.2 %finish.1 = bf16[192,2048]{1,0:T(8,128)(2,1)} custom-call(bf16[3072,128]{1,0:T(8,128)(2,1)} %bitcast.34, bf16[192,2048]{1,0:T(8,128)(2,1)} %bitcast.25, bf16[1,2048]{1,0:T(2,128)(2,1)} %broadcast_in_dim.3.gain_ref, bf16[344,2048]{1,0:T(8,128)(2,1)} %bitcast.22, bf16[344,2048]{1,0:T(8,128)(2,1)} %bitcast.23, bf16[344,2048]{1,0:T(8,128)(2,1)} %w_down_hbm.1, ...), custom_call_target="tpu_custom_call" | custom-call | flops 14596177920 | bytes 16777216 | tf_op jit(solution)/shard_map/finish/pallas_call | solution.py:692
  288.4 2.1 copy.27
Async XLA Ops:
  100.7 28.9 %copy-start = (bf16[2048]{0:T(1024)(128)(2,1)S(1)}, bf16[2048]{0:T(1024)(128)(2,1)}, u32[]{:S(2)}) copy-start(bf16[2048]{0:T(1024)(128)(2,1)} %param.34) | copy-start | bytes 12292

commit v6 on v5

--- a/solution.py
+++ b/solution.py
@@ -25,6 +25,11 @@
 def scaled_norm(wide_vals, gain):
     inv_rms = lax.rsqrt(jnp.mean(wide_vals * wide_vals, axis=-1, keepdims=True) + NORM_EPS)
     return (wide_vals * inv_rms * gain).astype(jnp.bfloat16)
+
+
+def flat_gain(ref):
+    wide = ref[...].astype(jnp.float32)
+    return jnp.concatenate([wide[i:i + 1, :] for i in range(wide.shape[0])], axis=1)
 
 
 def place():
@@ -272,7 +277,7 @@
     weights.keep().start()
     for load in loads:
         load.start()
-    rows_buf[own, :] = scaled_norm(x_ref[...].astype(jnp.float32), gain_ref[...].astype(jnp.float32))
+    rows_buf[own, :] = scaled_norm(x_ref[...].astype(jnp.float32), flat_gain(gain_ref))
     meet(where)
     gather = RowGather(rows_buf, send_sem, recv_sem, where, weights)
     gather.start()
@@ -352,7 +357,7 @@
         compiler_params=pltpu.CompilerParams(collective_id=0, has_side_effects=True, vmem_limit_bytes=62 * 2**20),
         cost_estimate=pl.CostEstimate(flops=2 * 16 * rows * width * 3 * head_dim, bytes_accessed=4 * rows * width, transcendentals=0),
         name="project",
-    )(x_rows.reshape(rows, width), gain.reshape(1, width), w_q, w_k, w_v, *biases, prefix, coarse_cos, coarse_sin, step_cos, step_sin, w_o)
+    )(x_rows.reshape(rows, width), gain.reshape(width // 128, 128), w_q, w_k, w_v, *biases, prefix, coarse_cos, coarse_sin, step_cos, step_sin, w_o)
     return tuple(o.reshape(16, n_req, own_tokens, head_dim) for o in outs), w_o_full
 
 
@@ -525,7 +530,7 @@
         out = jnp.dot(attended[...], part[pl.ds(0, w_o_ref.shape[0]), cols], preferred_element_type=jnp.float32).astype(jnp.bfloat16)
         resid[:, cols] = (x_ref[:, cols].astype(jnp.float32) + out.astype(jnp.float32)).astype(jnp.bfloat16)
 
-    rows_buf[block_rows(me), :] = scaled_norm(resid[...].astype(jnp.float32), gain_ref[...].astype(jnp.float32))
+    rows_buf[block_rows(me), :] = scaled_norm(resid[...].astype(jnp.float32), flat_gain(gain_ref))
     gather = RowGather(rows_buf, gather_send, gather_recv, where)
     gather.start()
     for mlp_load in mlp_loads:
@@ -711,7 +716,7 @@
         compiler_params=pltpu.CompilerParams(collective_id=1, has_side_effects=True, vmem_limit_bytes=62 * 2**20),
         cost_estimate=pl.CostEstimate(flops=2 * rows * width * (width + 16 * 3 * w_down.shape[0]), bytes_accessed=4 * width * width, transcendentals=0),
         name="finish",
-    )(attended.reshape(16 * rows, head_dim), x_rows.reshape(rows, width), gain[None, :], w_gate.T, w_up.T, w_down, w_o)
+    )(attended.reshape(16 * rows, head_dim), x_rows.reshape(rows, width), gain.reshape(width // 128, 128), w_gate.T, w_up.T, w_down, w_o)
     return out.reshape(x_rows.shape)
 
 

time: 289 us -> 285 us (0.986)
  Pallas kernels: 286 us -> 283 us
where the time goes in v6:
time: 285 us; the launch traced here: 286 us
  Pallas kernels  283 us (99%)
    pallas_call x1, Pallas kernels, finish(): pl.pallas_call(finish_body, out_shape=jax.ShapeDtypeStruct((rows, width),...  158 us
    pallas_call x1, Pallas kernels, project_all(): pl.pallas_call(project_body, out_shape=(out, out, out, jax.ShapeDtypeStru...  98.8 us
    pallas_call x1, Pallas kernels, attend(): pl.pallas_call(attention_body, out_shape=(jax.ShapeDtypeStruct(queries.sh...  26.4 us

profile of v6, /device:TPU:0, one launch (start us, length us, event | category | flops | bytes accessed | tf_op | source)
XLA Modules:
  0.0 286.2 jit_solution(5064346575186517720)
XLA Ops:
  0.6 98.8 %project.1 = (bf16[3072,128]{1,0:T(8,128)(2,1)}, bf16[3072,128]{1,0:T(8,128)(2,1)}, bf16[3072,128]{1,0:T(8,128)(2,1)}, bf16[2048,2048]{1,0:T(8,128)(2,1)}) custom-call(bf16[192,2048]{1,0:T(8,128)(2,1)} %bitcast.26, bf16[16,128]{1,0:T(8,128)(2,1)} %bitcast.28, bf16[2048,128]{1,0:T(8,128)(2,1)} %wq_ref.1, bf16[2048,128]{1,0:T(8,128)(2,1)} %wk_ref.1, ...), custom_call_target="tpu_custom_call" | custom-call | flops 4831838208 | bytes 1572864 | tf_op jit(solution)/shard_map/project/pallas_call | solution.py:345
  99.5 26.4 %attend.1 = (bf16[16,8,24,128]{3,2,1,0:T(8,128)(2,1)}, bf16[8,4096,128]{2,1,0:T(8,128)(2,1)}, bf16[8,4096,128]{2,1,0:T(8,128)(2,1)}) custom-call(s32[8]{0:T(128)} %prefix_ref.3, s32[8]{0:T(128)} %valid_ref.1, bf16[16,8,24,128]{3,2,1,0:T(8,128)(2,1)} %bitcast.35, bf16[16,8,24,128]{3,2,1,0:T(8,128)(2,1)} %bitcast.36, bf16[16,8,24,128]{3,2,1,0:T(8,128)(2,1)} %bitcast.37, ...), custom_call_target="tpu_custom_call" | custom-call | flops 6442450944 | bytes 33554432 | tf_op jit(solution)/shard_map/attend/pallas_call | solution.py:463
  125.9 158.2 %finish.1 = bf16[192,2048]{1,0:T(8,128)(2,1)} custom-call(bf16[3072,128]{1,0:T(8,128)(2,1)} %bitcast.38, bf16[192,2048]{1,0:T(8,128)(2,1)} %bitcast.27, bf16[16,128]{1,0:T(8,128)(2,1)} %bitcast.29, bf16[344,2048]{1,0:T(8,128)(2,1)} %bitcast.24, bf16[344,2048]{1,0:T(8,128)(2,1)} %bitcast.25, bf16[344,2048]{1,0:T(8,128)(2,1)} %w_down_hbm.1, ...), custom_call_target="tpu_custom_call" | custom-call | flops 14596177920 | bytes 16777216 | tf_op jit(solution)/shard_map/finish/pallas_call | solution.py:697
  284.1 2.1 copy.27
